TPU v7x, 32 devices: a 4x4x1 block of a 4x4x8 slice. The times are simulated.
32 devices in a mesh: batch: 1 (over z), row: 4 (over y), col: 8 (over x, core).
Axes of the slice: x: 4, y: 4, z: 1, core: 2. Of those that a mesh axis runs over, the one named last changes fastest.
The devices are a block of a 4x4x8 slice.
Arguments:
- left_op: bfloat16 [3072, 3072], P(('batch', 'row'), 'col')
- left_start: float32 [3072, 384], P(('batch', 'row', 'col'))
- right_op: bfloat16 [8192, 8192], P(('batch', 'row'), 'col')
- right_start: float32 [8192, 384], P(('batch', 'row', 'col'))
Outputs:
- output 1: float32 [3072, 384], P(('batch', 'row', 'col'))
- output 2: float32 [384, 384], P('batch')
- output 3: float32 [8192, 384], P(('batch', 'row', 'col'))
- output 4: float32 [384, 384], P('batch')
All inputs are finite; a program needn't handle non-finite values.
Results may differ from a plain program's by a relative error of at most 0.00100245.
Values are sent between devices in bfloat16 or wider.
A program may use at most 768 MiB of HBM per device.

v0:
```python
import jax
import jax.numpy as jnp
from jax import lax
from jax.sharding import PartitionSpec as P

SWEEPS = 4
ROW_CONTRACT = (((0,), (0,)), ((), ()))


def gram_total(lhs_mat, rhs_mat, precision, grid_axes):
    local_gram = lax.dot_general(lhs_mat, rhs_mat, ROW_CONTRACT, precision=precision, preferred_element_type=jnp.float32)
    return lax.psum(local_gram, grid_axes)


def cholqr_step(y_mat, gram_mat):
    chol_low = jnp.linalg.cholesky(gram_mat)
    return lax.linalg.triangular_solve(chol_low, y_mat, left_side=False, lower=True, transpose_a=True)


def orthonormalize(y_sub, total_rows, grid_axes):
    y_half = y_sub.astype(jnp.bfloat16)
    gram_one = gram_total(y_half, y_half, None, grid_axes) / total_rows
    y_one = cholqr_step(y_sub, gram_one)
    gram_two = gram_total(y_one, y_one, lax.Precision.HIGHEST, grid_axes) / total_rows
    return cholqr_step(y_one, gram_two)


def solution(mesh):
    row_size = mesh.shape["row"]
    col_size = mesh.shape["col"]
    grid_axes = ("row", "col")
    perm_pairs = [(src_index, (src_index % row_size) * col_size + src_index // row_size) for src_index in range(row_size * col_size)]

    def apply_op(op_blk, x_sub):
        x_moved = lax.ppermute(x_sub.astype(jnp.bfloat16), grid_axes, perm_pairs)
        x_col = lax.all_gather(x_moved, "row", axis=0, tiled=True)
        partial_prod = jnp.dot(op_blk, x_col, preferred_element_type=jnp.float32)
        return lax.psum_scatter(partial_prod, "col", scatter_dimension=0, tiled=True)

    def iterate_local(op_blk, start_sub):
        total_rows = op_blk.shape[0] * row_size
        x_sub = start_sub
        for sweep_index in range(SWEEPS):
            x_sub = orthonormalize(apply_op(op_blk, x_sub), total_rows, grid_axes)
        z_sub = apply_op(op_blk, x_sub)
        rayleigh = gram_total(x_sub, z_sub, lax.Precision.HIGHEST, grid_axes) / total_rows
        return x_sub, rayleigh

    def local_program(left_op, left_start, right_op, right_start):
        left_basis, left_rayleigh = iterate_local(left_op, left_start)
        right_basis, right_rayleigh = iterate_local(right_op, right_start)
        return left_basis, left_rayleigh, right_basis, right_rayleigh

    op_spec = P(("batch", "row"), "col")
    vec_spec = P(("batch", "row", "col"), None)
    small_spec = P("batch", None)
    return jax.shard_map(local_program, mesh=mesh, in_specs=(op_spec, vec_spec, op_spec, vec_spec), out_specs=(vec_spec, small_spec, vec_spec, small_spec), check_vma=False)
```

profile of v0, /device:TPU:97, one launch (start us, length us, event | category | flops | bytes accessed | tf_op | source)
XLA Modules:
  0.0 2924.3 jit_solution(1748163826777170296)
XLA Ops:
  16.6 13.6 all_gather.30
  43.3 18.3 all_gather.35
  70.0 31.8 %reduce-scatter.21.cloned.1.call-done = f32[256,384]{1,0:T(8,128)} async-done(((f32[2048,384]{1,0:T(8,128)}), f32[256,384]{1,0:T(8,128)}) %reduce-scatter.21.cloned.1.call-update) | async-done | bytes 393232 | tf_op jit(solution)/shard_map/reduce_scatter | solution.py:38
  104.4 99.1 %all-reduce.36.cloned.1.call-done = (f32[384,384]{0,1:T(8,128)}, f32[384,384]{0,1:T(8,128)}) async-done(((f32[384,384]{0,1:T(8,128)}, f32[384,384]{0,1:T(8,128)}), (f32[384,384]{0,1:T(8,128)}, f32[384,384]{0,1:T(8,128)})) %all-reduce.36.cloned.1.call-update) | async-done | bytes 1179664 | tf_op jit(solution)/shard_map/psum | solution.py:12
  231.2 11.7 cholesky.1137
  254.3 11.7 cholesky.1156
  276.1 29.9 %custom-call.66 = f32[3,128,128]{1,2,0:T(8,128)S(1)} custom-call(f32[3,128,128]{2,1,0:T(8,128)S(1)} %get-tuple-element.107), custom_call_target="InvertDiagBlocksLowerTriangular" | custom-call | tf_op jit(solution)/shard_map/triangular_solve/custom-call.2 | solution.py:17
  330.9 11.7 cholesky.1561
  353.1 11.7 cholesky.1580
  374.9 29.5 %custom-call.90 = f32[3,128,128]{1,2,0:T(8,128)S(1)} custom-call(f32[3,128,128]{2,1,0:T(8,128)S(1)} %get-tuple-element.115), custom_call_target="InvertDiagBlocksLowerTriangular" | custom-call | tf_op jit(solution)/shard_map/triangular_solve/custom-call.6 | solution.py:17
  408.3 94.9 %all-reduce.34.cloned.1.call-done = (f32[384,384]{0,1:T(8,128)}, f32[384,384]{0,1:T(8,128)}) async-done(((f32[384,384]{0,1:T(8,128)}, f32[384,384]{0,1:T(8,128)}), (f32[384,384]{0,1:T(8,128)}, f32[384,384]{0,1:T(8,128)})) %all-reduce.34.cloned.1.call-update) | async-done | bytes 1179664 | tf_op jit(solution)/shard_map/psum | solution.py:12
  505.8 11.7 cholesky.1171
  527.9 11.7 cholesky.1190
  550.4 11.7 cholesky.1209
  572.0 29.5 %custom-call.69 = f32[3,128,128]{1,2,0:T(8,128)S(1)} custom-call(f32[3,128,128]{2,1,0:T(8,128)S(1)} %get-tuple-element.108), custom_call_target="InvertDiagBlocksLowerTriangular" | custom-call | tf_op jit(solution)/shard_map/triangular_solve/custom-call.2 | solution.py:17
  606.0 11.7 cholesky.1595
  628.2 11.7 cholesky.1614
  650.6 11.7 cholesky.1633
  685.1 29.5 %custom-call.93 = f32[3,128,128]{1,2,0:T(8,128)S(1)} custom-call(f32[3,128,128]{2,1,0:T(8,128)S(1)} %get-tuple-element.116), custom_call_target="InvertDiagBlocksLowerTriangular" | custom-call | tf_op jit(solution)/shard_map/triangular_solve/custom-call.6 | solution.py:17
  730.7 13.0 all_gather.36
  751.7 30.7 %reduce-scatter.23.cloned.1.call-done = f32[256,384]{0,1:T(8,128)} async-done(((f32[2048,384]{0,1:T(8,128)}), f32[256,384]{0,1:T(8,128)}) %reduce-scatter.23.cloned.1.call-update) | async-done | bytes 393232 | tf_op jit(solution)/shard_map/reduce_scatter | solution.py:38
  784.9 99.0 %all-reduce.32.cloned.1.call-done = (f32[384,384]{0,1:T(8,128)}, f32[384,384]{0,1:T(8,128)}) async-done(((f32[384,384]{0,1:T(8,128)}, f32[384,384]{0,1:T(8,128)}), (f32[384,384]{0,1:T(8,128)}, f32[384,384]{0,1:T(8,128)})) %all-reduce.32.cloned.1.call-update) | async-done | bytes 1179664 | tf_op jit(solution)/shard_map/psum | solution.py:12
  886.4 11.7 cholesky.1224
  908.6 11.7 cholesky.1243
  930.9 11.7 cholesky.1262
  952.5 29.9 %custom-call.72 = f32[3,128,128]{1,2,0:T(8,128)S(1)} custom-call(f32[3,128,128]{2,1,0:T(8,128)S(1)} %get-tuple-element.109), custom_call_target="InvertDiagBlocksLowerTriangular" | custom-call | tf_op jit(solution)/shard_map/triangular_solve/custom-call.2 | solution.py:17
  985.6 11.7 cholesky.1648
  1007.8 11.7 cholesky.1667
  1030.0 11.7 cholesky.1686
  1051.8 29.5 %custom-call.96 = f32[3,128,128]{1,2,0:T(8,128)S(1)} custom-call(f32[3,128,128]{2,1,0:T(8,128)S(1)} %get-tuple-element.117), custom_call_target="InvertDiagBlocksLowerTriangular" | custom-call | tf_op jit(solution)/shard_map/triangular_solve/custom-call.6 | solution.py:17
  1084.8 95.0 %all-reduce.30.cloned.1.call-done = (f32[384,384]{0,1:T(8,128)}, f32[384,384]{0,1:T(8,128)}) async-done(((f32[384,384]{0,1:T(8,128)}, f32[384,384]{0,1:T(8,128)}), (f32[384,384]{0,1:T(8,128)}, f32[384,384]{0,1:T(8,128)})) %all-reduce.30.cloned.1.call-update) | async-done | bytes 1179664 | tf_op jit(solution)/shard_map/psum | solution.py:12
  1182.3 11.7 cholesky.1277
  1204.5 11.7 cholesky.1296
  1226.9 11.7 cholesky.1315
  1248.5 29.5 %custom-call.75 = f32[3,128,128]{1,2,0:T(8,128)S(1)} custom-call(f32[3,128,128]{2,1,0:T(8,128)S(1)} %get-tuple-element.110), custom_call_target="InvertDiagBlocksLowerTriangular" | custom-call | tf_op jit(solution)/shard_map/triangular_solve/custom-call.2 | solution.py:17
  1282.5 11.7 cholesky.1701
  1304.7 11.7 cholesky.1720
  1327.2 11.7 cholesky.1739
  1361.7 29.5 %custom-call.99 = f32[3,128,128]{1,2,0:T(8,128)S(1)} custom-call(f32[3,128,128]{2,1,0:T(8,128)S(1)} %get-tuple-element.118), custom_call_target="InvertDiagBlocksLowerTriangular" | custom-call | tf_op jit(solution)/shard_map/triangular_solve/custom-call.6 | solution.py:17
  1407.3 13.1 all_gather.37
  1428.3 30.7 %reduce-scatter.25.cloned.1.call-done = f32[256,384]{0,1:T(8,128)} async-done(((f32[2048,384]{0,1:T(8,128)}), f32[256,384]{0,1:T(8,128)}) %reduce-scatter.25.cloned.1.call-update) | async-done | bytes 393232 | tf_op jit(solution)/shard_map/reduce_scatter | solution.py:38
  1461.5 98.9 %all-reduce.28.cloned.1.call-done = (f32[384,384]{0,1:T(8,128)}, f32[384,384]{0,1:T(8,128)}) async-done(((f32[384,384]{0,1:T(8,128)}, f32[384,384]{0,1:T(8,128)}), (f32[384,384]{0,1:T(8,128)}, f32[384,384]{0,1:T(8,128)})) %all-reduce.28.cloned.1.call-update) | async-done | bytes 1179664 | tf_op jit(solution)/shard_map/psum | solution.py:12
  1563.0 11.7 cholesky.1330
  1585.2 11.7 cholesky.1349
  1607.4 11.7 cholesky.1368
  1629.0 29.9 %custom-call.78 = f32[3,128,128]{1,2,0:T(8,128)S(1)} custom-call(f32[3,128,128]{2,1,0:T(8,128)S(1)} %get-tuple-element.111), custom_call_target="InvertDiagBlocksLowerTriangular" | custom-call | tf_op jit(solution)/shard_map/triangular_solve/custom-call.2 | solution.py:17
  1662.1 11.7 cholesky.1754
  1684.3 11.7 cholesky.1773
  1706.5 11.7 cholesky.1792
  1728.3 29.5 %custom-call.102 = f32[3,128,128]{1,2,0:T(8,128)S(1)} custom-call(f32[3,128,128]{2,1,0:T(8,128)S(1)} %get-tuple-element.119), custom_call_target="InvertDiagBlocksLowerTriangular" | custom-call | tf_op jit(solution)/shard_map/triangular_solve/custom-call.6 | solution.py:17
  1761.3 94.9 %all-reduce.26.cloned.1.call-done = (f32[384,384]{0,1:T(8,128)}, f32[384,384]{0,1:T(8,128)}) async-done(((f32[384,384]{0,1:T(8,128)}, f32[384,384]{0,1:T(8,128)}), (f32[384,384]{0,1:T(8,128)}, f32[384,384]{0,1:T(8,128)})) %all-reduce.26.cloned.1.call-update) | async-done | bytes 1179664 | tf_op jit(solution)/shard_map/psum | solution.py:12
  1925.0 29.5 %custom-call.81 = f32[3,128,128]{1,2,0:T(8,128)S(1)} custom-call(f32[3,128,128]{2,1,0:T(8,128)S(1)} %get-tuple-element.112), custom_call_target="InvertDiagBlocksLowerTriangular" | custom-call | tf_op jit(solution)/shard_map/triangular_solve/custom-call.2 | solution.py:17
  2038.1 29.5 %custom-call.105 = f32[3,128,128]{1,2,0:T(8,128)S(1)} custom-call(f32[3,128,128]{2,1,0:T(8,128)S(1)} %get-tuple-element.120), custom_call_target="InvertDiagBlocksLowerTriangular" | custom-call | tf_op jit(solution)/shard_map/triangular_solve/custom-call.6 | solution.py:17
  2083.7 13.0 all_gather.38
  2104.7 30.7 %reduce-scatter.27.cloned.1.call-done = f32[256,384]{0,1:T(8,128)} async-done(((f32[2048,384]{0,1:T(8,128)}), f32[256,384]{0,1:T(8,128)}) %reduce-scatter.27.cloned.1.call-update) | async-done | bytes 393232 | tf_op jit(solution)/shard_map/reduce_scatter | solution.py:38
  2137.9 98.8 %all-reduce.24.cloned.1.call-done = (f32[384,384]{0,1:T(8,128)}, f32[384,384]{0,1:T(8,128)}) async-done(((f32[384,384]{0,1:T(8,128)}, f32[384,384]{0,1:T(8,128)}), (f32[384,384]{0,1:T(8,128)}, f32[384,384]{0,1:T(8,128)})) %all-reduce.24.cloned.1.call-update) | async-done | bytes 1179664 | tf_op jit(solution)/shard_map/psum | solution.py:12
  2305.3 29.9 %custom-call.84 = f32[3,128,128]{1,2,0:T(8,128)S(1)} custom-call(f32[3,128,128]{2,1,0:T(8,128)S(1)} %get-tuple-element.113), custom_call_target="InvertDiagBlocksLowerTriangular" | custom-call | tf_op jit(solution)/shard_map/triangular_solve/custom-call.2 | solution.py:17
  2404.6 29.5 %custom-call.108 = f32[3,128,128]{1,2,0:T(8,128)S(1)} custom-call(f32[3,128,128]{2,1,0:T(8,128)S(1)} %get-tuple-element.121), custom_call_target="InvertDiagBlocksLowerTriangular" | custom-call | tf_op jit(solution)/shard_map/triangular_solve/custom-call.6 | solution.py:17
  2437.7 95.0 %all-reduce.22.cloned.1.call-done = (f32[384,384]{0,1:T(8,128)}, f32[384,384]{0,1:T(8,128)}) async-done(((f32[384,384]{0,1:T(8,128)}, f32[384,384]{0,1:T(8,128)}), (f32[384,384]{0,1:T(8,128)}, f32[384,384]{0,1:T(8,128)})) %all-reduce.22.cloned.1.call-update) | async-done | bytes 1179664 | tf_op jit(solution)/shard_map/psum | solution.py:12
  2601.5 29.5 %custom-call.87 = f32[3,128,128]{1,2,0:T(8,128)S(1)} custom-call(f32[3,128,128]{2,1,0:T(8,128)S(1)} %get-tuple-element.114), custom_call_target="InvertDiagBlocksLowerTriangular" | custom-call | tf_op jit(solution)/shard_map/triangular_solve/custom-call.2 | solution.py:17
  2714.4 29.5 %custom-call.111 = f32[3,128,128]{1,2,0:T(8,128)S(1)} custom-call(f32[3,128,128]{2,1,0:T(8,128)S(1)} %get-tuple-element.122), custom_call_target="InvertDiagBlocksLowerTriangular" | custom-call | tf_op jit(solution)/shard_map/triangular_solve/custom-call.6 | solution.py:17
  2760.0 13.0 all_gather.39
  2781.3 30.4 %reduce-scatter.29.cloned.1.call-done = f32[256,384]{0,1:T(8,128)} async-done(((f32[2048,384]{0,1:T(8,128)}), f32[256,384]{0,1:T(8,128)}) %reduce-scatter.29.cloned.1.call-update) | async-done | bytes 393232 | tf_op jit(solution)/shard_map/reduce_scatter | solution.py:38
  2815.3 97.9 %all-reduce.20.cloned.1.call-done = (f32[384,384]{0,1:T(8,128)}, f32[384,384]{0,1:T(8,128)}) async-done(((f32[384,384]{0,1:T(8,128)}, f32[384,384]{0,1:T(8,128)}), (f32[384,384]{0,1:T(8,128)}, f32[384,384]{0,1:T(8,128)})) %all-reduce.20.cloned.1.call-update) | async-done | bytes 1179664 | tf_op jit(solution)/shard_map/psum | solution.py:12
  (735 shorter events, 1058.2 us)
Async XLA Ops:
  7.2 23.1 copy-start
  7.2 24.7 copy-start.17
  7.2 60.7 %reduce-scatter.19.cloned.1.call-start = ((), (), s32[]{:S(2)}) async-start(), calls=%async_computation.10 | async-start | bytes 1327104 | tf_op jit(solution)/shard_map/reduce_scatter | solution.py:38
  8.3 8.4 collective-permute-start
  31.8 70.0 %reduce-scatter.21.cloned.1.call-start = ((), (), s32[]{:S(2)}) async-start(), calls=%async_computation.11 | async-start | bytes 3538944 | tf_op jit(solution)/shard_map/reduce_scatter | solution.py:38
  32.0 11.3 collective-permute-start.5
  67.8 135.6 %all-reduce.36.cloned.1.call-start = ((), (), s32[]{:S(2)}) async-start(), calls=%async_computation.28 | async-start | bytes 2359296 | tf_op jit(solution)/shard_map/psum | solution.py:12
  104.1 399.1 %all-reduce.34.cloned.1.call-start = ((), (), s32[]{:S(2)}) async-start(), calls=%async_computation.27 | async-start | bytes 2359296 | tf_op jit(solution)/shard_map/psum | solution.py:12
  203.4 2.8 copy-start.8
  203.4 2.8 copy-start.9
  206.4 0.8 copy-start.10
  206.4 99.6 %copy-start.16 = (f32[96,384]{1,0:T(8,128)S(1)}, f32[96,384]{1,0:T(8,128)}, u32[]{:S(2)}) copy-start(f32[96,384]{1,0:T(8,128)} %reduce-scatter.19.cloned.1.call-done) | copy-start | bytes 442372
  306.7 97.7 %copy-start.11 = (f32[256,384]{1,0:T(8,128)S(1)}, f32[256,384]{1,0:T(8,128)}, u32[]{:S(2)}) copy-start(f32[256,384]{1,0:T(8,128)} %reduce-scatter.21.cloned.1.call-done) | copy-start | bytes 1179652
  408.0 341.5 %reduce-scatter.31.cloned.1.call-start = ((), (), s32[]{:S(2)}) async-start(), calls=%async_computation.16 | async-start | bytes 1327104
  505.7 99.9 %copy-start.2 = (f32[384,384]{0,1:T(8,128)S(1)}, f32[384,384]{0,1:T(8,128)}, u32[]{:S(2)}) copy-start(f32[384,384]{0,1:T(8,128)} %get-tuple-element.274) | copy-start | bytes 1769476
  602.6 63.6 %collective-permute-start.1 = (bf16[96,384]{1,0:T(8,128)(2,1)S(1)}, bf16[96,384]{1,0:T(8,128)(2,1)S(1)}, u32[]{:S(2)}, u32[]{:S(2)}) collective-permute-start(bf16[96,384]{1,0:T(8,128)(2,1)S(1)} %maximum_convert_fusion.3), channel_id=1, source_target_pairs={{0,0},{1,8},{2,16},{3,24},{4,1},{5,9},{6,17},{7,25},{8,2},{9,10},{... | collective-permute-start | bytes 221192 | tf_op jit(solution)/shard_map/ppermute | solution.py:35
  679.0 103.4 %reduce-scatter.23.cloned.1.call-start = ((), (), s32[]{:S(2)}) async-start(), calls=%async_computation.12 | async-start | bytes 3538944 | tf_op jit(solution)/shard_map/reduce_scatter | solution.py:38
  716.2 14.5 collective-permute-start.6
  749.5 134.4 %all-reduce.32.cloned.1.call-start = ((), (), s32[]{:S(2)}) async-start(), calls=%async_computation.26 | async-start | bytes 2359296 | tf_op jit(solution)/shard_map/psum | solution.py:12
  784.6 395.2 %all-reduce.30.cloned.1.call-start = ((), (), s32[]{:S(2)}) async-start(), calls=%async_computation.25 | async-start | bytes 2359296 | tf_op jit(solution)/shard_map/psum | solution.py:12
  898.2 87.0 %copy-start.5 = (f32[384,384]{0,1:T(8,128)S(1)}, f32[384,384]{0,1:T(8,128)}, u32[]{:S(2)}) copy-start(f32[384,384]{0,1:T(8,128)} %get-tuple-element.272) | copy-start | bytes 1769476
  985.5 95.8 %copy-start.12 = (f32[256,384]{0,1:T(8,128)S(1)}, f32[256,384]{0,1:T(8,128)}, u32[]{:S(2)}) copy-start(f32[256,384]{0,1:T(8,128)} %reduce-scatter.23.cloned.1.call-done) | copy-start | bytes 1179652
  1084.5 341.6 %reduce-scatter.33.cloned.1.call-start = ((), (), s32[]{:S(2)}) async-start(), calls=%async_computation.17 | async-start | bytes 1327104
  1182.3 99.9 %copy-start.3 = (f32[384,384]{0,1:T(8,128)S(1)}, f32[384,384]{0,1:T(8,128)}, u32[]{:S(2)}) copy-start(f32[384,384]{0,1:T(8,128)} %get-tuple-element.270) | copy-start | bytes 1769476
  1279.2 63.6 %collective-permute-start.2 = (bf16[96,384]{1,0:T(8,128)(2,1)S(1)}, bf16[96,384]{1,0:T(8,128)(2,1)S(1)}, u32[]{:S(2)}, u32[]{:S(2)}) collective-permute-start(bf16[96,384]{1,0:T(8,128)(2,1)S(1)} %maximum_convert_fusion.4), channel_id=1, source_target_pairs={{0,0},{1,8},{2,16},{3,24},{4,1},{5,9},{6,17},{7,25},{8,2},{9,10},{... | collective-permute-start | bytes 221192 | tf_op jit(solution)/shard_map/ppermute | solution.py:35
  1355.6 103.4 %reduce-scatter.25.cloned.1.call-start = ((), (), s32[]{:S(2)}) async-start(), calls=%async_computation.13 | async-start | bytes 3538944 | tf_op jit(solution)/shard_map/reduce_scatter | solution.py:38
  1392.7 14.5 collective-permute-start.7
  1426.1 134.3 %all-reduce.28.cloned.1.call-start = ((), (), s32[]{:S(2)}) async-start(), calls=%async_computation.24 | async-start | bytes 2359296 | tf_op jit(solution)/shard_map/psum | solution.py:12
  1461.2 395.0 %all-reduce.26.cloned.1.call-start = ((), (), s32[]{:S(2)}) async-start(), calls=%async_computation.23 | async-start | bytes 2359296 | tf_op jit(solution)/shard_map/psum | solution.py:12
  1574.8 87.0 %copy-start.6 = (f32[384,384]{0,1:T(8,128)S(1)}, f32[384,384]{0,1:T(8,128)}, u32[]{:S(2)}) copy-start(f32[384,384]{0,1:T(8,128)} %get-tuple-element.268) | copy-start | bytes 1769476
  1662.0 95.8 %copy-start.13 = (f32[256,384]{0,1:T(8,128)S(1)}, f32[256,384]{0,1:T(8,128)}, u32[]{:S(2)}) copy-start(f32[256,384]{0,1:T(8,128)} %reduce-scatter.25.cloned.1.call-done) | copy-start | bytes 1179652
  1761.1 341.5 %reduce-scatter.35.cloned.1.call-start = ((), (), s32[]{:S(2)}) async-start(), calls=%async_computation.18 | async-start | bytes 1327104
  1858.8 99.9 %copy-start.4 = (f32[384,384]{0,1:T(8,128)S(1)}, f32[384,384]{0,1:T(8,128)}, u32[]{:S(2)}) copy-start(f32[384,384]{0,1:T(8,128)} %get-tuple-element.266) | copy-start | bytes 1769476
  1955.6 63.6 %collective-permute-start.3 = (bf16[96,384]{1,0:T(8,128)(2,1)S(1)}, bf16[96,384]{1,0:T(8,128)(2,1)S(1)}, u32[]{:S(2)}, u32[]{:S(2)}) collective-permute-start(bf16[96,384]{1,0:T(8,128)(2,1)S(1)} %maximum_convert_fusion.5), channel_id=1, source_target_pairs={{0,0},{1,8},{2,16},{3,24},{4,1},{5,9},{6,17},{7,25},{8,2},{9,10},{... | collective-permute-start | bytes 221192 | tf_op jit(solution)/shard_map/ppermute | solution.py:35
  2032.0 103.4 %reduce-scatter.27.cloned.1.call-start = ((), (), s32[]{:S(2)}) async-start(), calls=%async_computation.14 | async-start | bytes 3538944 | tf_op jit(solution)/shard_map/reduce_scatter | solution.py:38
  2069.2 14.5 collective-permute-start.8
  2102.5 134.3 %all-reduce.24.cloned.1.call-start = ((), (), s32[]{:S(2)}) async-start(), calls=%async_computation.22 | async-start | bytes 2359296 | tf_op jit(solution)/shard_map/psum | solution.py:12
  2137.7 395.0 %all-reduce.22.cloned.1.call-start = ((), (), s32[]{:S(2)}) async-start(), calls=%async_computation.21 | async-start | bytes 2359296 | tf_op jit(solution)/shard_map/psum | solution.py:12
  2251.1 87.0 %copy-start.7 = (f32[384,384]{0,1:T(8,128)S(1)}, f32[384,384]{0,1:T(8,128)}, u32[]{:S(2)}) copy-start(f32[384,384]{0,1:T(8,128)} %get-tuple-element.264) | copy-start | bytes 1769476
  2338.3 95.8 %copy-start.14 = (f32[256,384]{0,1:T(8,128)S(1)}, f32[256,384]{0,1:T(8,128)}, u32[]{:S(2)}) copy-start(f32[256,384]{0,1:T(8,128)} %reduce-scatter.27.cloned.1.call-done) | copy-start | bytes 1179652
  2437.4 341.5 %reduce-scatter.37.cloned.1.call-start = ((), (), s32[]{:S(2)}) async-start(), calls=%async_computation.19 | async-start | bytes 1327104
  2535.2 100.0 %copy-start.1 = (f32[384,384]{0,1:T(8,128)S(1)}, f32[384,384]{0,1:T(8,128)}, u32[]{:S(2)}) copy-start(f32[384,384]{0,1:T(8,128)} %get-tuple-element.262) | copy-start | bytes 1769476
  2632.2 146.8 %copy-start.15 = (f32[96,384]{1,0:T(8,128)}, f32[96,384]{1,0:T(8,128)S(1)}, u32[]{:S(2)}) copy-start(f32[96,384]{1,0:T(8,128)S(1)} %get-tuple-element.278) | copy-start | bytes 442372
  2632.2 63.4 %collective-permute-start.4 = (bf16[96,384]{1,0:T(8,128)(2,1)S(1)}, bf16[96,384]{1,0:T(8,128)(2,1)S(1)}, u32[]{:S(2)}, u32[]{:S(2)}) collective-permute-start(bf16[96,384]{1,0:T(8,128)(2,1)S(1)} %get-tuple-element.277), channel_id=1, source_target_pairs={{0,0},{1,8},{2,16},{3,24},{4,1},{5,9},{6,17},{7,25},{8,2},{9,10},{... | collective-permute-start | bytes 221192 | tf_op jit(solution)/shard_map/ppermute | solution.py:35
  2708.3 103.4 %reduce-scatter.29.cloned.1.call-start = ((), (), s32[]{:S(2)}) async-start(), calls=%async_computation.15 | async-start | bytes 3538944 | tf_op jit(solution)/shard_map/reduce_scatter | solution.py:38
  2745.5 14.5 collective-permute-start.9
  2778.8 134.4 %all-reduce.20.cloned.1.call-start = ((), (), s32[]{:S(2)}) async-start(), calls=%async_computation.20 | async-start | bytes 2359296 | tf_op jit(solution)/shard_map/psum | solution.py:12
Sparse Core Ops, SparseCore 0:
  32.0 31.2 reduce-scatter.18
  68.0 33.8 reduce-scatter.20
  105.8 97.5 all-reduce.35
  408.1 95.0 all-reduce.33
  679.1 29.7 reduce-scatter.30
  749.6 32.7 reduce-scatter.22
  786.3 97.5 all-reduce.31
  1084.7 95.0 all-reduce.29
  1355.7 29.6 reduce-scatter.32
  1426.2 32.7 reduce-scatter.24
  1462.9 97.4 all-reduce.27
  1761.2 94.9 all-reduce.25
  2032.1 29.6 reduce-scatter.34
  2102.6 32.7 reduce-scatter.26
  2139.2 97.4 all-reduce.23
  2437.5 95.0 all-reduce.21
  2708.4 29.6 reduce-scatter.36
  2778.9 32.7 reduce-scatter.28
  2815.6 97.5 all-reduce.19
where the time goes:
time: 2930 us; the launch traced here: 2920 us
  other arithmetic  1410 us (48%)
  waiting for transfers between devices  1070 us (37%)
  blocking collectives  127 us (4%)
  local copies, waits for them, and re-layouts  112 us (4%)
  matrix products  105 us (4%)
  starting transfers between devices  55.5 us (2%)
  between operations  48 us (2%)
    another operation x176, other arithmetic, cholqr_step(): chol_low = jnp.linalg.cholesky(gram_mat)  913 us
    psum x9, waiting for transfers between devices, gram_total(): return lax.psum(local_gram, grid_axes)  873 us
    another operation x34, other arithmetic, cholqr_step(): lax.linalg.triangular_solve(chol_low, y_mat, left_side=False, lower=True,...  474 us
    reduce_scatter x6, waiting for transfers between devices, apply_op(): lax.psum_scatter(partial_prod, 'col', scatter_dimension=0, tiled=True)  154 us
    all_gather x10, blocking collectives, apply_op(): x_col = lax.all_gather(x_moved, 'row', axis=0, tiled=True)  127 us
    another operation x161, local copies, waits for them, and re-layouts, cholqr_step(): lax.linalg.triangular_solve(chol_low, y_mat, left_side=False, lower=True,...  95.3 us
  transfers between devices with their start and end apart: 29, of which 20 were waited for; matrix products, arithmetic and copies ran while one was open for 14% of the time, Pallas kernels for 0%

commit v1 on v0

v1 whole, which is shorter than its diff:
```python
import functools

import jax
import jax.numpy as jnp
from jax import lax
from jax.experimental import pallas as pl
from jax.experimental.pallas import tpu as pltpu
from jax.sharding import PartitionSpec as P

SWEEPS = 4
ROW_CONTRACT = (((0,), (0,)), ((), ()))
LANE_CONTRACT = (((1,), (1,)), ((), ()))

LN=128; PAN=32; SL=8
HI=lax.Precision.HIGHEST
def bl(x, j):
    return jnp.broadcast_to(x[:, j:j+1], (SL, LN))
def bs(x, k):
    return jnp.broadcast_to(x[k:k+1, :], (SL, LN))


def panel(b_ref, w_ref, m, P, nt):
    q = P*PAN//LN
    r0 = P*PAN
    G = PAN//SL
    tB = list(range(q, nt)); tW = list(range(0, q+1))
    B = [[b_ref[m, r0+g*SL:r0+(g+1)*SL, t*LN:(t+1)*LN] for t in tB] for g in range(G)]
    W = [[w_ref[m, r0+g*SL:r0+(g+1)*SL, t*LN:(t+1)*LN] for t in tW] for g in range(G)]
    sub = lax.broadcasted_iota(jnp.int32, (SL, LN), 0)
    gens = []
    for s in range(G):
        c0 = (r0 + s*SL) % LN
        C = [[bl(B[g][0], c0+k) for k in range(SL)] for g in range(s, G)]
        yield
        for k in range(SL):
            p = bs(C[0][k], k)
            rs = lax.rsqrt(p)
            rowB = [bs(x, k)*rs for x in B[s]]
            rowW = [bs(x, k)*rs for x in W[s]]
            crow = {kk: bs(C[0][kk], k)*rs for kk in range(k+1, SL)}
            for gi, g in enumerate(range(s, G)):
                mm = C[gi][k]*rs
                if gi == 0:
                    keep = sub == k
                    mm = jnp.where(sub > k, mm, 0.0)
                    B[g] = [jnp.where(keep, rb, x - mm*rb) for x, rb in zip(B[g], rowB)]
                    W[g] = [jnp.where(keep, rb, x - mm*rb) for x, rb in zip(W[g], rowW)]
                else:
                    B[g] = [x - mm*rb for x, rb in zip(B[g], rowB)]
                    W[g] = [x - mm*rb for x, rb in zip(W[g], rowW)]
                for kk in range(k+1, SL):
                    C[gi][kk] = C[gi][kk] - mm*crow[kk]
            yield
        for i, t in enumerate(tB):
            b_ref[m, r0+s*SL:r0+(s+1)*SL, t*LN:(t+1)*LN] = B[s][i]
        for i, t in enumerate(tW):
            w_ref[m, r0+s*SL:r0+(s+1)*SL, t*LN:(t+1)*LN] = W[s][i]
    yield
    n = nt*LN
    r1 = r0+PAN
    if r1 < n:
        for qq in range(r1//LN, nt):
            lo = max(r1, qq*LN); hi = (qq+1)*LN
            a = b_ref[m, r0:r1, qq*LN:hi]
            at = a.T[lo-qq*LN:, :]
            rhsB = b_ref[m, r0:r1, qq*LN:n]
            b_ref[m, lo:hi, qq*LN:n] = b_ref[m, lo:hi, qq*LN:n] - jnp.dot(at, rhsB, precision=HI, preferred_element_type=jnp.float32)
            rhsW = w_ref[m, r0:r1, 0:(q+1)*LN]
            w_ref[m, lo:hi, 0:(q+1)*LN] = w_ref[m, lo:hi, 0:(q+1)*LN] - jnp.dot(at, rhsW, precision=HI, preferred_element_type=jnp.float32)

def chol_body(scales, g_ref, w_ref, b_ref):
    nm, n, _ = g_ref.shape
    nt = n//LN
    r = lax.broadcasted_iota(jnp.int32, (n, n), 0); c = lax.broadcasted_iota(jnp.int32, (n, n), 1)
    for m in range(nm):
        b_ref[m] = g_ref[m]*scales[m]
        w_ref[m] = jnp.where(r == c, 1.0, 0.0).astype(jnp.float32)
    for pan in range(n//PAN):
        its = [panel(b_ref, w_ref, m, pan, nt) for m in range(nm)]
        done = False
        while not done:
            for it in its:
                try: next(it)
                except StopIteration: done = True

def chol_inv(g, scales):
    nm, n, _ = g.shape
    return pl.pallas_call(functools.partial(chol_body, scales),
        out_shape=jax.ShapeDtypeStruct((nm, n, n), jnp.float32),
        in_specs=[pl.BlockSpec(memory_space=pltpu.VMEM)], out_specs=pl.BlockSpec(memory_space=pltpu.VMEM),
        scratch_shapes=[pltpu.VMEM((nm, n, n), jnp.float32)],
        name="chol_inv")(g)


def gram(lhs_mat, rhs_mat, precision):
    return lax.dot_general(lhs_mat, rhs_mat, ROW_CONTRACT, precision=precision, preferred_element_type=jnp.float32)


def times_rinv(y_mat, l_inv):
    return lax.dot_general(y_mat, l_inv, LANE_CONTRACT, precision=HI, preferred_element_type=jnp.float32)


def solution(mesh):
    row_size = mesh.shape["row"]
    col_size = mesh.shape["col"]
    grid_axes = ("row", "col")
    perm_pairs = [(src_index, (src_index % row_size) * col_size + src_index // row_size) for src_index in range(row_size * col_size)]

    def apply_op(op_blk, x_sub):
        x_moved = lax.ppermute(x_sub.astype(jnp.bfloat16), grid_axes, perm_pairs)
        x_col = lax.all_gather(x_moved, "row", axis=0, tiled=True)
        partial_prod = jnp.dot(op_blk, x_col, preferred_element_type=jnp.float32)
        return lax.psum_scatter(partial_prod, "col", scatter_dimension=0, tiled=True)

    def local_program(left_op, left_start, right_op, right_start):
        scales = (1.0 / (left_op.shape[0] * row_size), 1.0 / (right_op.shape[0] * row_size))

        def normalize(ys, hs, precision):
            grams = lax.psum(jnp.stack([gram(h, h, precision) for h in hs]), grid_axes)
            l_inv = chol_inv(grams, scales)
            return tuple(times_rinv(y, l_inv[i]) for i, y in enumerate(ys))

        def sweep(_, xs):
            ys = (apply_op(left_op, xs[0]), apply_op(right_op, xs[1]))
            ys = normalize(ys, tuple(y.astype(jnp.bfloat16) for y in ys), None)
            return normalize(ys, ys, HI)

        xs = lax.fori_loop(0, SWEEPS, sweep, (left_start, right_start))
        zs = (apply_op(left_op, xs[0]), apply_op(right_op, xs[1]))
        ray = lax.psum(jnp.stack([gram(x, z, HI) for x, z in zip(xs, zs)]), grid_axes)
        return xs[0], ray[0] * scales[0], xs[1], ray[1] * scales[1]

    op_spec = P(("batch", "row"), "col")
    vec_spec = P(("batch", "row", "col"), None)
    small_spec = P("batch", None)
    return jax.shard_map(local_program, mesh=mesh, in_specs=(op_spec, vec_spec, op_spec, vec_spec), out_specs=(vec_spec, small_spec, vec_spec, small_spec), check_vma=False)
```

time: 2930 us -> 1570 us (0.54)
  other arithmetic: 1410 us -> 12.4 us
  Pallas kernels: 0 us -> 160 us
  local copies, waits for them, and re-layouts: 112 us -> 3.38 us
  between operations: 48 us -> 15.8 us
    another operation x210 -> x9, other arithmetic: 1390 us -> 9.9 us  [the longest x8 8.8 us: normalize(): grams = lax.psum(jnp.stack([gram(h, h, precision) for h in hs]), grid_axes)]
    pallas_call x0 -> x8, Pallas kernels: none -> 160 us  [chol_inv(): pl.pallas_call(functools.partial(chol_body, scales), out_shape=jax.ShapeD...]
    another operation x209 -> x0, local copies, waits for them, and re-layouts: 96.1 us -> none  [the longest x161 95.3 us: cholqr_step(): lax.linalg.triangular_solve(chol_low, y_mat, left_side=False, lower=True,...]
    another operation x144 -> x0, matrix products: 40.9 us -> none  [the longest x80 22 us: cholqr_step(): lax.linalg.triangular_solve(chol_low, y_mat, left_side=False, lower=True,...]
    reduce_scatter x6 -> x9, waiting for transfers between devices: 154 us -> 156 us  [apply_op(): lax.psum_scatter(partial_prod, 'col', scatter_dimension=0, tiled=True)]
  transfers between devices with their start and end apart: 29 -> 29, of which waited for: 20 -> 24; matrix products, arithmetic and copies ran while one was open for 14% -> 2% of each run, Pallas kernels for 0% -> 0%
where the time goes in v1:
time: 1570 us; the launch traced here: 1560 us
  waiting for transfers between devices  1090 us (69%)
  Pallas kernels  160 us (10%)
  blocking collectives  145 us (9%)
  matrix products  89.2 us (6%)
  starting transfers between devices  44 us (3%)
  between operations  15.8 us (1%)
    psum x8, waiting for transfers between devices, normalize(): grams = lax.psum(jnp.stack([gram(h, h, precision) for h in hs]), grid_axes)  772 us
    pallas_call x8, Pallas kernels, chol_inv(): pl.pallas_call(functools.partial(chol_body, scales), out_shape=jax.ShapeD...  160 us
    reduce_scatter x9, waiting for transfers between devices, apply_op(): lax.psum_scatter(partial_prod, 'col', scatter_dimension=0, tiled=True)  156 us
    all_gather x10, blocking collectives, apply_op(): x_col = lax.all_gather(x_moved, 'row', axis=0, tiled=True)  145 us
    psum x1, waiting for transfers between devices, local_program(): lax.psum(jnp.stack([gram(x, z, HI) for x, z in zip(xs, zs)]), grid_axes)  97.5 us
    ppermute x10, waiting for transfers between devices, apply_op(): x_moved = lax.ppermute(x_sub.astype(jnp.bfloat16), grid_axes, perm_pairs)  61.2 us
    dot_general x10, matrix products, apply_op(): partial_prod = jnp.dot(op_blk, x_col, preferred_element_type=jnp.float32)  42.3 us
    ppermute x10, starting transfers between devices, apply_op(): x_moved = lax.ppermute(x_sub.astype(jnp.bfloat16), grid_axes, perm_pairs)  41.8 us
  transfers between devices with their start and end apart: 29, of which 24 were waited for; matrix products, arithmetic and copies ran while one was open for 2% of the time, Pallas kernels for 0%

profile of v1, /device:TPU:97, one launch (start us, length us, event | category | flops | bytes accessed | tf_op | source)
XLA Modules:
  0.0 1564.9 jit_solution(15153063916138620535)
XLA Ops:
  9.9 1353.4 %while.12 = (s32[]{:T(128)}, f32[96,384]{1,0:T(8,128)S(1)}, f32[256,384]{1,0:T(8,128)S(1)}, bf16[768,384]{1,0:T(8,128)(2,1)}, bf16[2048,1024]{1,0:T(8,128)(2,1)}, /*index=5*/s32[]{:T(128)}) while((s32[]{:T(128)}, f32[96,384]{1,0:T(8,128)S(1)}, f32[256,384]{1,0:T(8,128)S(1)}, bf16[768,384]{1,0:T(8,128)(2,1)}, bf16[2048,1024]{1,0:T(8,128)(2,1)}, ...), condition=%wide.region_5.0_spmd, body=%wide.region_0.0_spmd.sunk | while | flops 3810926592 | bytes 61751688 | solution.py:128
  10.0 5.1 collective-permute-start
  15.1 3.3 collective-permute-done
  18.3 13.6 all_gather.16
  31.9 2.6 fusion.64
  34.7 5.2 collective-permute-start.1
  39.9 6.2 collective-permute-done.1
  46.1 18.3 %all_gather.17 = bf16[1024,384]{1,0:T(8,128)(2,1)S(1)} all-gather(bf16[256,384]{1,0:T(8,128)(2,1)S(1)} %collective-permute-done.1), channel_id=1, replica_groups=mesh['batch'=1,'row'=4,'col'=8] {'row'}, dimensions={0}, use_global_device_ids=true | all-gather | bytes 983040 | tf_op jit(solution)/shard_map/while/body/eval_jaxpr/all_gather | solution.py:111
  64.3 6.2 fusion.65
  71.9 32.7 %reduce-scatter.13.cloned.1.call-done = f32[256,384]{1,0:T(8,128)} async-done(((f32[2048,384]{1,0:T(8,128)}), f32[256,384]{1,0:T(8,128)}) %reduce-scatter.13.cloned.1.call-update) | async-done | bytes 393232 | tf_op jit(solution)/shard_map/while/body/eval_jaxpr/reduce_scatter | solution.py:113
  107.4 98.0 %all-reduce.6.cloned.1.call-done.g_ref = f32[2,384,384]{2,1,0:T(8,128)} async-done(((f32[2,384,384]{2,1,0:T(8,128)}), f32[2,384,384]{2,1,0:T(8,128)}) %all-reduce.6.cloned.1.call-update) | async-done | bytes 1179664 | tf_op jit(solution)/shard_map/while/body/eval_jaxpr/psum | solution.py:119
  205.4 20.0 %chol_inv.2 = f32[2,384,384]{2,1,0:T(8,128)} custom-call(f32[2,384,384]{2,1,0:T(8,128)} %all-reduce.6.cloned.1.call-done.g_ref), custom_call_target="tpu_custom_call" | custom-call | tf_op jit(solution)/shard_map/while/body/eval_jaxpr/chol_inv/pallas_call | solution.py:88
  230.9 95.1 %all-reduce.8.cloned.1.call-done.g_ref = f32[2,384,384]{2,1,0:T(8,128)} async-done(((f32[2,384,384]{2,1,0:T(8,128)}), f32[2,384,384]{2,1,0:T(8,128)}) %all-reduce.8.cloned.1.call-update) | async-done | bytes 1179664 | tf_op jit(solution)/shard_map/while/body/eval_jaxpr/psum | solution.py:119
  326.0 20.2 %chol_inv.3 = f32[2,384,384]{2,1,0:T(8,128)} custom-call(f32[2,384,384]{2,1,0:T(8,128)} %all-reduce.8.cloned.1.call-done.g_ref), custom_call_target="tpu_custom_call" | custom-call | tf_op jit(solution)/shard_map/while/body/eval_jaxpr/chol_inv/pallas_call | solution.py:88
  350.2 2.8 collective-permute-start
  353.1 5.2 collective-permute-done
  358.2 11.5 all_gather.16
  369.7 2.6 fusion.64
  372.5 5.1 collective-permute-start.1
  377.6 7.8 collective-permute-done.1
  385.4 16.8 %all_gather.17 = bf16[1024,384]{1,0:T(8,128)(2,1)S(1)} all-gather(bf16[256,384]{1,0:T(8,128)(2,1)S(1)} %collective-permute-done.1), channel_id=1, replica_groups=mesh['batch'=1,'row'=4,'col'=8] {'row'}, dimensions={0}, use_global_device_ids=true | all-gather | bytes 983040 | tf_op jit(solution)/shard_map/while/body/eval_jaxpr/all_gather | solution.py:111
  402.2 6.2 fusion.65
  409.8 31.0 %reduce-scatter.13.cloned.1.call-done = f32[256,384]{1,0:T(8,128)} async-done(((f32[2048,384]{1,0:T(8,128)}), f32[256,384]{1,0:T(8,128)}) %reduce-scatter.13.cloned.1.call-update) | async-done | bytes 393232 | tf_op jit(solution)/shard_map/while/body/eval_jaxpr/reduce_scatter | solution.py:113
  443.6 98.0 %all-reduce.6.cloned.1.call-done.g_ref = f32[2,384,384]{2,1,0:T(8,128)} async-done(((f32[2,384,384]{2,1,0:T(8,128)}), f32[2,384,384]{2,1,0:T(8,128)}) %all-reduce.6.cloned.1.call-update) | async-done | bytes 1179664 | tf_op jit(solution)/shard_map/while/body/eval_jaxpr/psum | solution.py:119
  541.6 20.2 %chol_inv.2 = f32[2,384,384]{2,1,0:T(8,128)} custom-call(f32[2,384,384]{2,1,0:T(8,128)} %all-reduce.6.cloned.1.call-done.g_ref), custom_call_target="tpu_custom_call" | custom-call | tf_op jit(solution)/shard_map/while/body/eval_jaxpr/chol_inv/pallas_call | solution.py:88
  567.3 95.0 %all-reduce.8.cloned.1.call-done.g_ref = f32[2,384,384]{2,1,0:T(8,128)} async-done(((f32[2,384,384]{2,1,0:T(8,128)}), f32[2,384,384]{2,1,0:T(8,128)}) %all-reduce.8.cloned.1.call-update) | async-done | bytes 1179664 | tf_op jit(solution)/shard_map/while/body/eval_jaxpr/psum | solution.py:119
  662.3 19.9 %chol_inv.3 = f32[2,384,384]{2,1,0:T(8,128)} custom-call(f32[2,384,384]{2,1,0:T(8,128)} %all-reduce.8.cloned.1.call-done.g_ref), custom_call_target="tpu_custom_call" | custom-call | tf_op jit(solution)/shard_map/while/body/eval_jaxpr/chol_inv/pallas_call | solution.py:88
  686.4 2.8 collective-permute-start
  689.2 5.1 collective-permute-done
  694.4 11.5 all_gather.16
  705.9 2.6 fusion.64
  708.7 5.0 collective-permute-start.1
  713.7 7.8 collective-permute-done.1
  721.5 16.8 %all_gather.17 = bf16[1024,384]{1,0:T(8,128)(2,1)S(1)} all-gather(bf16[256,384]{1,0:T(8,128)(2,1)S(1)} %collective-permute-done.1), channel_id=1, replica_groups=mesh['batch'=1,'row'=4,'col'=8] {'row'}, dimensions={0}, use_global_device_ids=true | all-gather | bytes 983040 | tf_op jit(solution)/shard_map/while/body/eval_jaxpr/all_gather | solution.py:111
  738.3 6.2 fusion.65
  745.9 31.0 %reduce-scatter.13.cloned.1.call-done = f32[256,384]{1,0:T(8,128)} async-done(((f32[2048,384]{1,0:T(8,128)}), f32[256,384]{1,0:T(8,128)}) %reduce-scatter.13.cloned.1.call-update) | async-done | bytes 393232 | tf_op jit(solution)/shard_map/while/body/eval_jaxpr/reduce_scatter | solution.py:113
  779.9 97.8 %all-reduce.6.cloned.1.call-done.g_ref = f32[2,384,384]{2,1,0:T(8,128)} async-done(((f32[2,384,384]{2,1,0:T(8,128)}), f32[2,384,384]{2,1,0:T(8,128)}) %all-reduce.6.cloned.1.call-update) | async-done | bytes 1179664 | tf_op jit(solution)/shard_map/while/body/eval_jaxpr/psum | solution.py:119
  877.8 19.9 %chol_inv.2 = f32[2,384,384]{2,1,0:T(8,128)} custom-call(f32[2,384,384]{2,1,0:T(8,128)} %all-reduce.6.cloned.1.call-done.g_ref), custom_call_target="tpu_custom_call" | custom-call | tf_op jit(solution)/shard_map/while/body/eval_jaxpr/chol_inv/pallas_call | solution.py:88
  903.2 95.0 %all-reduce.8.cloned.1.call-done.g_ref = f32[2,384,384]{2,1,0:T(8,128)} async-done(((f32[2,384,384]{2,1,0:T(8,128)}), f32[2,384,384]{2,1,0:T(8,128)}) %all-reduce.8.cloned.1.call-update) | async-done | bytes 1179664 | tf_op jit(solution)/shard_map/while/body/eval_jaxpr/psum | solution.py:119
  998.3 20.0 %chol_inv.3 = f32[2,384,384]{2,1,0:T(8,128)} custom-call(f32[2,384,384]{2,1,0:T(8,128)} %all-reduce.8.cloned.1.call-done.g_ref), custom_call_target="tpu_custom_call" | custom-call | tf_op jit(solution)/shard_map/while/body/eval_jaxpr/chol_inv/pallas_call | solution.py:88
  1022.5 2.8 collective-permute-start
  1025.4 5.2 collective-permute-done
  1030.5 11.5 all_gather.16
  1042.0 2.6 fusion.64
  1044.8 5.1 collective-permute-start.1
  1049.9 7.8 collective-permute-done.1
  1057.7 16.8 %all_gather.17 = bf16[1024,384]{1,0:T(8,128)(2,1)S(1)} all-gather(bf16[256,384]{1,0:T(8,128)(2,1)S(1)} %collective-permute-done.1), channel_id=1, replica_groups=mesh['batch'=1,'row'=4,'col'=8] {'row'}, dimensions={0}, use_global_device_ids=true | all-gather | bytes 983040 | tf_op jit(solution)/shard_map/while/body/eval_jaxpr/all_gather | solution.py:111
  1074.5 6.2 fusion.65
  1082.1 31.1 %reduce-scatter.13.cloned.1.call-done = f32[256,384]{1,0:T(8,128)} async-done(((f32[2048,384]{1,0:T(8,128)}), f32[256,384]{1,0:T(8,128)}) %reduce-scatter.13.cloned.1.call-update) | async-done | bytes 393232 | tf_op jit(solution)/shard_map/while/body/eval_jaxpr/reduce_scatter | solution.py:113
  1116.0 97.9 %all-reduce.6.cloned.1.call-done.g_ref = f32[2,384,384]{2,1,0:T(8,128)} async-done(((f32[2,384,384]{2,1,0:T(8,128)}), f32[2,384,384]{2,1,0:T(8,128)}) %all-reduce.6.cloned.1.call-update) | async-done | bytes 1179664 | tf_op jit(solution)/shard_map/while/body/eval_jaxpr/psum | solution.py:119
  1213.9 20.0 %chol_inv.2 = f32[2,384,384]{2,1,0:T(8,128)} custom-call(f32[2,384,384]{2,1,0:T(8,128)} %all-reduce.6.cloned.1.call-done.g_ref), custom_call_target="tpu_custom_call" | custom-call | tf_op jit(solution)/shard_map/while/body/eval_jaxpr/chol_inv/pallas_call | solution.py:88
  1239.4 95.0 %all-reduce.8.cloned.1.call-done.g_ref = f32[2,384,384]{2,1,0:T(8,128)} async-done(((f32[2,384,384]{2,1,0:T(8,128)}), f32[2,384,384]{2,1,0:T(8,128)}) %all-reduce.8.cloned.1.call-update) | async-done | bytes 1179664 | tf_op jit(solution)/shard_map/while/body/eval_jaxpr/psum | solution.py:119
  1334.4 20.2 %chol_inv.3 = f32[2,384,384]{2,1,0:T(8,128)} custom-call(f32[2,384,384]{2,1,0:T(8,128)} %all-reduce.8.cloned.1.call-done.g_ref), custom_call_target="tpu_custom_call" | custom-call | tf_op jit(solution)/shard_map/while/body/eval_jaxpr/chol_inv/pallas_call | solution.py:88
  1363.5 2.8 collective-permute-start.2
  1366.3 5.2 collective-permute-done.2
  1371.5 11.5 all_gather.12
  1386.2 5.1 collective-permute-start.3
  1391.2 7.8 collective-permute-done.3
  1399.0 16.8 %all_gather.13 = bf16[1024,384]{1,0:T(8,128)(2,1)S(1)} all-gather(bf16[256,384]{1,0:T(8,128)(2,1)S(1)} %collective-permute-done.3), channel_id=1, replica_groups=mesh['batch'=1,'row'=4,'col'=8] {'row'}, dimensions={0}, use_global_device_ids=true | all-gather | bytes 983040 | tf_op jit(solution)/shard_map/all_gather | solution.py:111
  1415.8 5.7 convolution_bitcast_fusion.4
  1423.2 30.6 %reduce-scatter.7.cloned.1.call-done = f32[256,384]{0,1:T(8,128)} async-done(((f32[2048,384]{0,1:T(8,128)}), f32[256,384]{0,1:T(8,128)}) %reduce-scatter.7.cloned.1.call-update) | async-done | bytes 393232 | tf_op jit(solution)/shard_map/reduce_scatter | solution.py:113
  1453.8 2.4 convolution_bitcast_fusion.6
  1457.4 97.5 %all-reduce.4.cloned.1.call-done = f32[2,384,384]{2,1,0:T(8,128)} async-done(((f32[2,384,384]{2,1,0:T(8,128)}), f32[2,384,384]{2,1,0:T(8,128)}) %all-reduce.4.cloned.1.call-update) | async-done | bytes 1179664 | tf_op jit(solution)/shard_map/psum | solution.py:130
  1555.0 2.3 fusion.6
  (127 shorter events, 62.7 us)
Async XLA Ops:
  9.9 60.7 %reduce-scatter.11.cloned.1.call-start = ((), (), s32[]{:S(2)}) async-start(), calls=%async_computation.7 | async-start | bytes 1327104 | tf_op jit(solution)/shard_map/while/body/eval_jaxpr/reduce_scatter | solution.py:113
  10.0 8.4 collective-permute-start
  34.6 70.0 %reduce-scatter.13.cloned.1.call-start = ((), (), s32[]{:S(2)}) async-start(), calls=%async_computation.8 | async-start | bytes 3538944 | tf_op jit(solution)/shard_map/while/body/eval_jaxpr/reduce_scatter | solution.py:113
  34.7 11.4 collective-permute-start.1
  70.6 134.9 %all-reduce.6.cloned.1.call-start = ((), (), s32[]{:S(2)}) async-start(), calls=%async_computation.9 | async-start | bytes 2359296 | tf_op jit(solution)/shard_map/while/body/eval_jaxpr/psum | solution.py:119
  107.2 118.2 %copy-start.1 = (f32[256,384]{1,0:T(8,128)S(1)}, f32[256,384]{1,0:T(8,128)}, u32[]{:S(2)}) copy-start(f32[256,384]{1,0:T(8,128)} %reduce-scatter.13.cloned.1.call-done) | copy-start | bytes 1179652 | tf_op jit(solution)/shard_map/while
  107.2 218.8 %all-reduce.8.cloned.1.call-start = ((), (), s32[]{:S(2)}) async-start(), calls=%async_computation.10 | async-start | bytes 2359296 | tf_op jit(solution)/shard_map/while/body/eval_jaxpr/psum | solution.py:119
  225.4 2.9 copy-start
  225.4 2.9 copy-start.3
  350.2 58.4 %reduce-scatter.11.cloned.1.call-start = ((), (), s32[]{:S(2)}) async-start(), calls=%async_computation.7 | async-start | bytes 1327104 | tf_op jit(solution)/shard_map/while/body/eval_jaxpr/reduce_scatter | solution.py:113
  350.2 8.0 collective-permute-start
  372.4 68.4 %reduce-scatter.13.cloned.1.call-start = ((), (), s32[]{:S(2)}) async-start(), calls=%async_computation.8 | async-start | bytes 3538944 | tf_op jit(solution)/shard_map/while/body/eval_jaxpr/reduce_scatter | solution.py:113
  372.5 12.8 collective-permute-start.1
  408.4 133.2 %all-reduce.6.cloned.1.call-start = ((), (), s32[]{:S(2)}) async-start(), calls=%async_computation.9 | async-start | bytes 2359296 | tf_op jit(solution)/shard_map/while/body/eval_jaxpr/psum | solution.py:119
  443.3 118.5 %copy-start.1 = (f32[256,384]{1,0:T(8,128)S(1)}, f32[256,384]{1,0:T(8,128)}, u32[]{:S(2)}) copy-start(f32[256,384]{1,0:T(8,128)} %reduce-scatter.13.cloned.1.call-done) | copy-start | bytes 1179652 | tf_op jit(solution)/shard_map/while
  443.3 219.0 %all-reduce.8.cloned.1.call-start = ((), (), s32[]{:S(2)}) async-start(), calls=%async_computation.10 | async-start | bytes 2359296 | tf_op jit(solution)/shard_map/while/body/eval_jaxpr/psum | solution.py:119
  561.8 2.9 copy-start
  561.8 2.9 copy-start.3
  686.3 58.4 %reduce-scatter.11.cloned.1.call-start = ((), (), s32[]{:S(2)}) async-start(), calls=%async_computation.7 | async-start | bytes 1327104 | tf_op jit(solution)/shard_map/while/body/eval_jaxpr/reduce_scatter | solution.py:113
  686.4 8.0 collective-permute-start
  708.6 68.3 %reduce-scatter.13.cloned.1.call-start = ((), (), s32[]{:S(2)}) async-start(), calls=%async_computation.8 | async-start | bytes 3538944 | tf_op jit(solution)/shard_map/while/body/eval_jaxpr/reduce_scatter | solution.py:113
  708.7 12.8 collective-permute-start.1
  744.6 133.2 %all-reduce.6.cloned.1.call-start = ((), (), s32[]{:S(2)}) async-start(), calls=%async_computation.9 | async-start | bytes 2359296 | tf_op jit(solution)/shard_map/while/body/eval_jaxpr/psum | solution.py:119
  779.5 118.3 %copy-start.1 = (f32[256,384]{1,0:T(8,128)S(1)}, f32[256,384]{1,0:T(8,128)}, u32[]{:S(2)}) copy-start(f32[256,384]{1,0:T(8,128)} %reduce-scatter.13.cloned.1.call-done) | copy-start | bytes 1179652 | tf_op jit(solution)/shard_map/while
  779.5 218.8 %all-reduce.8.cloned.1.call-start = ((), (), s32[]{:S(2)}) async-start(), calls=%async_computation.10 | async-start | bytes 2359296 | tf_op jit(solution)/shard_map/while/body/eval_jaxpr/psum | solution.py:119
  897.7 2.9 copy-start
  897.7 2.9 copy-start.3
  1022.4 58.4 %reduce-scatter.11.cloned.1.call-start = ((), (), s32[]{:S(2)}) async-start(), calls=%async_computation.7 | async-start | bytes 1327104 | tf_op jit(solution)/shard_map/while/body/eval_jaxpr/reduce_scatter | solution.py:113
  1022.5 8.0 collective-permute-start
  1044.7 68.4 %reduce-scatter.13.cloned.1.call-start = ((), (), s32[]{:S(2)}) async-start(), calls=%async_computation.8 | async-start | bytes 3538944 | tf_op jit(solution)/shard_map/while/body/eval_jaxpr/reduce_scatter | solution.py:113
  1044.8 12.8 collective-permute-start.1
  1080.7 133.1 %all-reduce.6.cloned.1.call-start = ((), (), s32[]{:S(2)}) async-start(), calls=%async_computation.9 | async-start | bytes 2359296 | tf_op jit(solution)/shard_map/while/body/eval_jaxpr/psum | solution.py:119
  1115.7 118.2 %copy-start.1 = (f32[256,384]{1,0:T(8,128)S(1)}, f32[256,384]{1,0:T(8,128)}, u32[]{:S(2)}) copy-start(f32[256,384]{1,0:T(8,128)} %reduce-scatter.13.cloned.1.call-done) | copy-start | bytes 1179652 | tf_op jit(solution)/shard_map/while
  1115.7 218.7 %all-reduce.8.cloned.1.call-start = ((), (), s32[]{:S(2)}) async-start(), calls=%async_computation.10 | async-start | bytes 2359296 | tf_op jit(solution)/shard_map/while/body/eval_jaxpr/psum | solution.py:119
  1233.9 2.9 copy-start
  1233.9 2.9 copy-start.3
  1363.4 58.3 %copy-start.4 = (f32[96,384]{1,0:T(8,128)}, f32[96,384]{1,0:T(8,128)S(1)}, u32[]{:S(2)}) copy-start(f32[96,384]{1,0:T(8,128)S(1)} %get-tuple-element.28) | copy-start | bytes 442372
  1363.4 90.4 %copy-start.2 = (f32[256,384]{1,0:T(8,128)}, f32[256,384]{1,0:T(8,128)S(1)}, u32[]{:S(2)}) copy-start(f32[256,384]{1,0:T(8,128)S(1)} %get-tuple-element.30) | copy-start | bytes 1179652
  1363.4 58.2 %reduce-scatter.9.cloned.1.call-start = ((), (), s32[]{:S(2)}) async-start(), calls=%async_computation.6 | async-start | bytes 1327104
  1363.5 8.0 collective-permute-start.2
  1386.0 67.8 %reduce-scatter.7.cloned.1.call-start = ((), (), s32[]{:S(2)}) async-start(), calls=%async_computation.4 | async-start | bytes 3538944 | tf_op jit(solution)/shard_map/reduce_scatter | solution.py:113
  1386.2 12.9 collective-permute-start.3
  1421.5 133.4 %all-reduce.4.cloned.1.call-start = ((), (), s32[]{:S(2)}) async-start(), calls=%async_computation.5 | async-start | bytes 2359296 | tf_op jit(solution)/shard_map/psum | solution.py:130
Sparse Core Ops, SparseCore 0:
  34.7 31.2 reduce-scatter.10
  70.7 33.8 reduce-scatter.12
  108.0 97.4 all-reduce.5
  231.1 94.9 all-reduce.7
  372.5 31.7 reduce-scatter.10
  408.5 32.1 reduce-scatter.12
  444.1 97.4 all-reduce.5
  567.4 94.8 all-reduce.7
  708.7 31.7 reduce-scatter.10
  744.7 32.1 reduce-scatter.12
  780.3 97.4 all-reduce.5
  903.3 94.8 all-reduce.7
  1044.8 31.7 reduce-scatter.10
  1080.9 32.2 reduce-scatter.12
  1116.4 97.4 all-reduce.5
  1239.5 94.8 all-reduce.7
Sparse Core Ops, SparseCore 1:
  1386.1 31.7 reduce-scatter.8
  1421.6 32.1 reduce-scatter.6
  1457.5 97.4 all-reduce.3

commit v2 on v1

v2 whole, which is shorter than its diff:
```python
import functools

import jax
import jax.numpy as jnp
from jax import lax
from jax.experimental import pallas as pl
from jax.experimental.pallas import tpu as pltpu
from jax.sharding import PartitionSpec as P

SWEEPS = 4
GRAIN = 512
LN=128; PAN=32; SL=8
HI=lax.Precision.HIGHEST

def bl(x, j):
    return jnp.broadcast_to(x[:, j:j+1], (SL, LN))

def bs(x, k):
    return jnp.broadcast_to(x[k:k+1, :], (SL, LN))


def panel(b_ref, w_ref, m, P, nt):
    q = P*PAN//LN
    r0 = P*PAN
    G = PAN//SL
    tB = list(range(q, nt)); tW = list(range(0, q+1))
    B = [[b_ref[m, r0+g*SL:r0+(g+1)*SL, t*LN:(t+1)*LN] for t in tB] for g in range(G)]
    W = [[w_ref[m, r0+g*SL:r0+(g+1)*SL, t*LN:(t+1)*LN] for t in tW] for g in range(G)]
    sub = lax.broadcasted_iota(jnp.int32, (SL, LN), 0)
    gens = []
    for s in range(G):
        c0 = (r0 + s*SL) % LN
        C = [[bl(B[g][0], c0+k) for k in range(SL)] for g in range(s, G)]
        yield
        for k in range(SL):
            p = bs(C[0][k], k)
            rs = lax.rsqrt(p)
            rowB = [bs(x, k)*rs for x in B[s]]
            rowW = [bs(x, k)*rs for x in W[s]]
            crow = {kk: bs(C[0][kk], k)*rs for kk in range(k+1, SL)}
            for gi, g in enumerate(range(s, G)):
                mm = C[gi][k]*rs
                if gi == 0:
                    keep = sub == k
                    mm = jnp.where(sub > k, mm, 0.0)
                    B[g] = [jnp.where(keep, rb, x - mm*rb) for x, rb in zip(B[g], rowB)]
                    W[g] = [jnp.where(keep, rb, x - mm*rb) for x, rb in zip(W[g], rowW)]
                else:
                    B[g] = [x - mm*rb for x, rb in zip(B[g], rowB)]
                    W[g] = [x - mm*rb for x, rb in zip(W[g], rowW)]
                for kk in range(k+1, SL):
                    C[gi][kk] = C[gi][kk] - mm*crow[kk]
            yield
        for i, t in enumerate(tB):
            b_ref[m, r0+s*SL:r0+(s+1)*SL, t*LN:(t+1)*LN] = B[s][i]
        for i, t in enumerate(tW):
            w_ref[m, r0+s*SL:r0+(s+1)*SL, t*LN:(t+1)*LN] = W[s][i]
    yield
    n = nt*LN
    r1 = r0+PAN
    if r1 < n:
        for qq in range(r1//LN, nt):
            lo = max(r1, qq*LN); hi = (qq+1)*LN
            a = b_ref[m, r0:r1, qq*LN:hi]
            at = a.T[lo-qq*LN:, :]
            rhsB = b_ref[m, r0:r1, qq*LN:n]
            b_ref[m, lo:hi, qq*LN:n] = b_ref[m, lo:hi, qq*LN:n] - jnp.dot(at, rhsB, precision=HI, preferred_element_type=jnp.float32)
            rhsW = w_ref[m, r0:r1, 0:(q+1)*LN]
            w_ref[m, lo:hi, 0:(q+1)*LN] = w_ref[m, lo:hi, 0:(q+1)*LN] - jnp.dot(at, rhsW, precision=HI, preferred_element_type=jnp.float32)

MESH = pl.DeviceIdType.MESH
RING = 4


def where_am_i():
    row = lax.axis_index("row")
    col = lax.axis_index("col")
    return row, col // 2, col % 2


def rows_at(start, size):
    return pl.ds(pl.multiple_of(start, 8), size)


class Links:
    def __init__(self, send, recv):
        self.send, self.recv, self.used = send, recv, 0
        self.row, self.col_x, self.core = where_am_i()
        self.open = []
    def pos(self, axis):
        return self.row if axis == "y" else self.col_x
    def peer(self, axis, step):
        if axis == "core":
            return {"row": self.row, "col": self.col_x * 2 + (1 - self.core)}
        if axis == "y":
            return {"row": (self.row + step) % RING, "col": self.col_x * 2 + self.core}
        return {"row": self.row, "col": ((self.col_x + step) % RING) * 2 + self.core}
    def copy(self, src, dst, axis, step=0):
        slot = self.used
        self.used += 1
        desc = pltpu.make_async_remote_copy(src_ref=src, dst_ref=dst, send_sem=self.send.at[slot], recv_sem=self.recv.at[slot], device_id=self.peer(axis, step), device_id_type=MESH)
        desc.start()
        self.open.append(desc)
        return desc
    def greet(self, who):
        barrier = pltpu.get_barrier_semaphore()
        for axis, step in who:
            pl.semaphore_signal(barrier, inc=1, device_id=self.peer(axis, step), device_id_type=MESH)
        pl.semaphore_wait(barrier, len(who))
    def drain(self):
        for desc in self.open:
            desc.wait_send()


def total_kernel(g_ref, out_ref, r_a, acc, r_b, part, r_c, fin, send, recv):
    rows = g_ref.shape[0]
    half, quart = rows // 2, rows // 4
    big, small = quart // RING, quart // RING // RING
    net = Links(send, recv)
    core = net.core
    net.greet([("core", 0)] + [(a, s) for a in ("x", "y") for s in (1, 2, 3)])
    first, second = ("x", "y"), ("y", "x")
    steps = (2, 1, 3, 0)
    swap = {}
    for s in steps:
        for h in range(2):
            j = (net.pos(first[h]) + s) % RING
            off = h * quart + j * big
            swap[h, s] = net.copy(g_ref.at[rows_at((1 - core) * half + off, big)], r_a.at[rows_at(off, big)], "core")
    out_b = {}
    for s in steps:
        for h in range(2):
            j = (net.pos(first[h]) + s) % RING
            off = h * quart + j * big
            swap[h, s].wait_recv()
            acc[rows_at(off, big)] = g_ref[rows_at(core * half + off, big)] + r_a[rows_at(off, big)]
            if s:
                out_b[h, s] = net.copy(acc.at[rows_at(off, big)], r_b.at[h, s - 1], first[h], s)
    for h in range(2):
        tot = acc[rows_at(h * quart + net.pos(first[h]) * big, big)]
        for s in (1, 3, 2):
            out_b[h, s].wait_recv()
            tot = tot + r_b[h, s - 1]
        part[h] = tot
    out_c = {}
    for s in (2, 1, 3):
        for h in range(2):
            j = (net.pos(second[h]) + s) % RING
            out_c[h, s] = net.copy(part.at[h, rows_at(j * small, small)], r_c.at[h, s - 1], second[h], s)
    base = [core * half + h * quart + net.pos(first[h]) * big for h in range(2)]
    out_d = {}
    for h in range(2):
        mine = net.pos(second[h]) * small
        tot = part[h, rows_at(mine, small)]
        for s in (1, 3, 2):
            out_c[h, s].wait_recv()
            tot = tot + r_c[h, s - 1]
        fin[rows_at(base[h] + mine, small)] = tot
        at = rows_at(base[h] + mine, small)
        for s in (2, 1, 3):
            out_d[h, s] = net.copy(fin.at[at], fin.at[at], second[h], s)
    out_e, out_f = {}, []
    for h in range(2):
        for s in (1, 3, 2):
            out_d[h, s].wait_recv()
        at = rows_at(base[h], big)
        for s in (2, 1, 3):
            out_e[h, s] = net.copy(fin.at[at], fin.at[at], first[h], s)
        out_f.append(net.copy(fin.at[at], fin.at[at], "core"))
    for s in (1, 3, 2):
        for h in range(2):
            out_e[h, s].wait_recv()
            j = (net.pos(first[h]) + RING - s) % RING
            at = rows_at(core * half + h * quart + j * big, big)
            out_f.append(net.copy(fin.at[at], fin.at[at], "core"))
    for desc in out_f:
        desc.wait_recv()
    net.drain()
    out_ref[...] = fin[...]


def grid_total(g, collective_id):
    rows = g.shape[0]
    big = rows // 16
    n_copies = 8 + 6 + 6 + 6 + 6 + 8
    f32 = jnp.float32
    vm = pl.BlockSpec(memory_space=pltpu.VMEM)
    return pl.pallas_call(total_kernel, out_shape=jax.ShapeDtypeStruct(g.shape, f32), in_specs=[vm], out_specs=vm,
        scratch_shapes=[pltpu.VMEM((rows // 2, 128), f32), pltpu.VMEM((rows // 2, 128), f32), pltpu.VMEM((2, 3, big, 128), f32), pltpu.VMEM((2, big, 128), f32), pltpu.VMEM((2, 3, big // 4, 128), f32), pltpu.VMEM((rows, 128), f32),
            pltpu.SemaphoreType.DMA((n_copies,)), pltpu.SemaphoreType.DMA((n_copies,))],
        compiler_params=pltpu.CompilerParams(collective_id=collective_id, has_side_effects=True), name="grid_total")(g)

COL_PAIR = 2
TRI = ((0, 0), (0, 1), (0, 2), (1, 1), (1, 2), (2, 2))


class Product:
    def __init__(self, net, across, op, x, y, xg, prod, pair, relay, final):
        self.net, self.across = net, across
        self.op, self.x, self.y, self.xg, self.prod, self.pair, self.relay, self.final = op, x, y, xg, prod, pair, relay, final
        self.gat, self.red = ("y", "x") if across else ("x", "y")
        self.sub = x.shape[0]
        self.gpos, self.rpos = net.pos(self.gat), net.pos(self.red)

    def xrow(self, pos, core=None):
        core = self.net.core if core is None else core
        return pos * self.sub if self.across else (pos * COL_PAIR + core) * self.sub

    def at(self, pos, lo=0, size=None, core=None):
        return self.xg.at[rows_at(self.xrow(pos, core) + lo, self.sub if size is None else size)]

    def near(self, step):
        return (self.gpos + step) % RING

    def s0(self):
        own = self.at(self.gpos)
        self.to_r = self.net.copy(self.x, own, self.gat, 1)
        self.to_l = self.net.copy(self.x, own, self.gat, 3)
        self.cores = []
        if not self.across:
            self.cores.append(self.net.copy(self.x, own, "core"))
        self.xg[rows_at(self.xrow(self.gpos), self.sub), :] = self.x[...]

    def s1(self):
        hs = self.sub // 2
        self.to_r.wait_recv()
        ref = self.at(self.near(3), 0, hs)
        self.fw_r = self.net.copy(ref, ref, self.gat, 1)
        self.to_l.wait_recv()
        ref = self.at(self.near(1), hs, hs)
        self.fw_l = self.net.copy(ref, ref, self.gat, 3)
        if not self.across:
            for step in (3, 1):
                ref = self.at(self.near(step))
                self.cores.append(self.net.copy(ref, ref, "core"))

    def s2(self):
        hs = self.sub // 2
        self.fw_r.wait_recv()
        self.fw_l.wait_recv()
        if not self.across:
            ref = self.at(self.near(2))
            self.cores.append(self.net.copy(ref, ref, "core"))
            for desc in self.cores:
                desc.wait_recv()

    def chunk_row(self, step, core=None):
        pos = (self.rpos + step) % RING
        core = self.net.core if core is None else core
        return (pos * COL_PAIR + core) * self.sub if self.across else pos * self.sub

    def multiply(self, start):
        at = rows_at(start, self.sub)
        self.prod[at, :] = jnp.dot(self.op[at, :], self.xg[...], preferred_element_type=jnp.float32)

    def chunk(self, step, slot):
        if self.across:
            other = self.chunk_row(step, 1 - self.net.core)
            self.multiply(other)
            desc = self.net.copy(self.prod.at[rows_at(other, self.sub)], self.pair.at[slot], "core")
            mine = self.chunk_row(step)
            self.multiply(mine)
            return desc
        self.multiply(self.chunk_row(step))

    def settle(self, step, slot, desc):
        if desc is not None:
            desc.wait_recv()
            at = rows_at(self.chunk_row(step), self.sub)
            self.prod[at, :] = self.prod[at, :] + self.pair[slot]

    def half(self, step, h):
        return rows_at(self.chunk_row(step) + h * (self.sub // 2), self.sub // 2)

    def s3(self):
        self.p2 = self.chunk(2, 0)
        if self.across:
            self.p1 = self.chunk(1, 1)
        self.settle(2, 0, self.p2)
        self.rel_r = self.net.copy(self.prod.at[self.half(2, 0)], self.relay.at[0], self.red, 1)
        self.rel_l = self.net.copy(self.prod.at[self.half(2, 1)], self.relay.at[1], self.red, 3)

    def s4(self):
        hs = self.sub // 2
        if not self.across:
            self.p1 = self.chunk(1, 1)
        self.p3 = self.chunk(3, 2)
        self.settle(1, 1, self.p1)
        self.dir_r = self.net.copy(self.prod.at[self.half(1, 1)], self.final.at[0, hs:, :], self.red, 1)
        self.p0 = self.chunk(0, 3)
        self.settle(3, 2, self.p3)
        self.dir_l = self.net.copy(self.prod.at[self.half(3, 0)], self.final.at[1, :hs, :], self.red, 3)

    def s5(self):
        hs = self.sub // 2
        self.rel_r.wait_recv()
        at = self.half(1, 0)
        self.prod[at, :] = self.prod[at, :] + self.relay[0]
        self.sum_r = self.net.copy(self.prod.at[at], self.final.at[0, :hs, :], self.red, 1)
        self.rel_l.wait_recv()
        at = self.half(3, 1)
        self.prod[at, :] = self.prod[at, :] + self.relay[1]
        self.sum_l = self.net.copy(self.prod.at[at], self.final.at[1, hs:, :], self.red, 3)

    def s6(self):
        self.settle(0, 3, self.p0)
        for desc in (self.dir_r, self.dir_l, self.sum_r, self.sum_l):
            desc.wait_recv()
        self.y[...] = self.prod[rows_at(self.chunk_row(0), self.sub), :] + self.final[0] + self.final[1]


def apply_kernel(left_across, lop, lx, rop, rx, ly, ry, g_ref, lxg, lprod, lpair, lrelay, lfinal, rxg, rprod, rpair, rrelay, rfinal, send, recv):
    net = Links(send, recv)
    net.greet([("core", 0)] + [(a, s) for a in ("x", "y") for s in (1, 3)])
    right = Product(net, not left_across, rop, rx, ry, rxg, rprod, rpair, rrelay, rfinal)
    left = Product(net, left_across, lop, lx, ly, lxg, lprod, lpair, lrelay, lfinal)
    for stage in range(7):
        getattr(right, f"s{stage}")()
        getattr(left, f"s{stage}")()
    net.drain()
    for i, y in enumerate((ly, ry)):
        h = y[...].astype(jnp.bfloat16)
        for j, (a, b) in enumerate(TRI):
            g_ref[(i*6+j)*128:(i*6+j+1)*128, :] = lax.dot_general(h[:, a*128:(a+1)*128], h[:, b*128:(b+1)*128], (((0,), (0,)), ((), ())), preferred_element_type=jnp.float32)


def apply_pair(left_across, lop, lx, rop, rx, collective_id):
    f32, bf = jnp.float32, jnp.bfloat16
    s = lx.shape[1]
    vm = pl.BlockSpec(memory_space=pltpu.VMEM)
    scratch = []
    for op, x in ((lop, lx), (rop, rx)):
        sub = x.shape[0]
        scratch += [pltpu.VMEM((op.shape[1], s), bf), pltpu.VMEM((op.shape[0], s), f32), pltpu.VMEM((4, sub, s), f32), pltpu.VMEM((2, sub//2, s), f32), pltpu.VMEM((2, sub, s), f32)]
    n = 2*(2+2+6) + 4 + 4
    scratch += [pltpu.SemaphoreType.DMA((n,)), pltpu.SemaphoreType.DMA((n,))]
    return pl.pallas_call(functools.partial(apply_kernel, left_across),
        out_shape=(jax.ShapeDtypeStruct(lx.shape, f32), jax.ShapeDtypeStruct(rx.shape, f32), jax.ShapeDtypeStruct((12*128, 128), f32)),
        in_specs=[vm]*4, out_specs=(vm,)*3, scratch_shapes=scratch,
        compiler_params=pltpu.CompilerParams(collective_id=collective_id, has_side_effects=True, vmem_limit_bytes=48*1024*1024), name="apply_%s" % ("n" if left_across else "t"))(lop, lx, rop, rx)

ROW_CONTRACT = (((0,), (0,)), ((), ()))
LANE_CONTRACT = (((1,), (1,)), ((), ()))


def orth_kernel(last, scales, g_ref, ly, ry, lo, ro, extra_l, extra_r, w_ref, b_ref):
    nm, n, _ = w_ref.shape
    nt = n // LN
    r = lax.broadcasted_iota(jnp.int32, (n, n), 0)
    c = lax.broadcasted_iota(jnp.int32, (n, n), 1)
    for m in range(nm):
        for j, (a, b) in enumerate(TRI):
            at = (m * len(TRI) + j) * LN
            b_ref[m, a * LN:(a + 1) * LN, b * LN:(b + 1) * LN] = g_ref[at:at + LN, :] * scales[m]
        w_ref[m] = jnp.where(r == c, 1.0, 0.0).astype(jnp.float32)
    for pan in range(n // PAN):
        its = [panel(b_ref, w_ref, m, pan, nt) for m in range(nm)]
        done = False
        while not done:
            for it in its:
                try:
                    next(it)
                except StopIteration:
                    done = True
    for m, (y, o) in enumerate(((ly, lo), (ry, ro))):
        x = lax.dot_general(y[...], w_ref[m], LANE_CONTRACT, precision=HI, preferred_element_type=jnp.float32)
        o[...] = x
        if last:
            (extra_l, extra_r)[m][...] = x.astype(jnp.bfloat16)
        else:
            for j, (a, b) in enumerate(TRI):
                at = (m * len(TRI) + j) * LN
                extra_l[at:at + LN, :] = lax.dot_general(x[:, a * LN:(a + 1) * LN], x[:, b * LN:(b + 1) * LN], ROW_CONTRACT, precision=HI, preferred_element_type=jnp.float32)


def orth_first(scales, g_ref, ly, ry, lo, ro, g2, w_ref, b_ref):
    orth_kernel(False, scales, g_ref, ly, ry, lo, ro, g2, None, w_ref, b_ref)


def orth_second(scales, g_ref, ly, ry, lo, ro, lh, rh, w_ref, b_ref):
    orth_kernel(True, scales, g_ref, ly, ry, lo, ro, lh, rh, w_ref, b_ref)


def orth(last, scales, g, ly, ry):
    n = ly.shape[1]
    f32, bf = jnp.float32, jnp.bfloat16
    vm = pl.BlockSpec(memory_space=pltpu.VMEM)
    like = lambda v, t: jax.ShapeDtypeStruct(v.shape, t)
    extra = (like(ly, bf), like(ry, bf)) if last else (like(g, f32),)
    return pl.pallas_call(functools.partial(orth_second if last else orth_first, scales),
        out_shape=(like(ly, f32), like(ry, f32)) + extra,
        in_specs=[vm] * 3, out_specs=(vm,) * (2 + len(extra)),
        scratch_shapes=[pltpu.VMEM((2, n, n), f32), pltpu.VMEM((2, n, n), f32)],
        name="orth_second" if last else "orth_first")(g, ly, ry)


def solution(mesh):
    row_size = mesh.shape["row"]
    col_size = mesh.shape["col"]
    grid_axes = ("row", "col")
    to_cols = [(i, (i % row_size) * col_size + i // row_size) for i in range(row_size * col_size)]
    to_rows = [(b, a) for a, b in to_cols]

    def local_program(left_op, left_start, right_op, right_start):
        scales = (1.0 / (left_op.shape[0] * row_size), 1.0 / (right_op.shape[0] * row_size))
        left_t, right_t = left_op.T, right_op.T

        def normalize(ys, g):
            ly, ry, g2 = orth(False, scales, grid_total(g, 2), ys[0], ys[1])
            return orth(True, scales, grid_total(g2, 2), ly, ry)

        def two_sweeps(_, carry):
            lh, rh = carry[2:]
            ly, ry, g = apply_pair(True, left_op, lh, right_t, rh, 0)
            _, _, lh, rh = normalize((ly, ry), g)
            ly, ry, g = apply_pair(False, left_t, lh, right_op, rh, 1)
            return normalize((ly, ry), g)

        lh = lax.ppermute(left_start.astype(jnp.bfloat16), grid_axes, to_cols)
        carry = (left_start, right_start, lh, right_start.astype(jnp.bfloat16))
        lx_cols, rx, lh, rh = lax.fori_loop(0, SWEEPS // 2, two_sweeps, carry)
        lx = lax.ppermute(lx_cols, grid_axes, to_rows)
        rx_cols = lax.ppermute(rx, grid_axes, to_cols)
        lz, rz_cols, _ = apply_pair(True, left_op, lh, right_t, rh, 0)
        n = lx.shape[1]
        parts = []
        for x, z in ((lx, lz), (rx_cols, rz_cols)):
            for t in range(n // LN):
                parts.append(lax.dot_general(x, z[:, t * LN:(t + 1) * LN], ROW_CONTRACT, precision=HI, preferred_element_type=jnp.float32))
        rows = sum(part.shape[0] for part in parts)
        parts.append(jnp.zeros((-rows % GRAIN, LN), jnp.float32))
        ray = grid_total(jnp.concatenate(parts, axis=0), 3)[:rows]
        ray = ray.reshape(2, n // LN, n, LN).transpose(0, 2, 1, 3).reshape(2, n, n)
        return lx, ray[0] * scales[0], rx, ray[1] * scales[1]

    op_spec = P(("batch", "row"), "col")
    vec_spec = P(("batch", "row", "col"), None)
    small_spec = P("batch", None)
    return jax.shard_map(local_program, mesh=mesh, in_specs=(op_spec, vec_spec, op_spec, vec_spec), out_specs=(vec_spec, small_spec, vec_spec, small_spec), check_vma=False)
```

time: 1570 us -> 616 us (0.39)
  waiting for transfers between devices: 1090 us -> 0.01 us
  Pallas kernels: 160 us -> 562 us
  blocking collectives: 145 us -> 0 us
  matrix products: 89.2 us -> 3.85 us
  starting transfers between devices: 44 us -> 10.7 us
  local copies, waits for them, and re-layouts: 3.38 us -> 27.1 us
    psum x9 -> x0, waiting for transfers between devices: 869 us -> none  [the longest x8 772 us: normalize(): grams = lax.psum(jnp.stack([gram(h, h, precision) for h in hs]), grid_axes)]
    pallas_call x8 -> x22, Pallas kernels: 160 us -> 562 us  [the longest x9 215 us: grid_total(): pl.pallas_call(total_kernel, out_shape=jax.ShapeDtypeStruct(g.shape, f32)...]
    reduce_scatter x9 -> x0, waiting for transfers between devices: 156 us -> none  [apply_op(): lax.psum_scatter(partial_prod, 'col', scatter_dimension=0, tiled=True)]
    all_gather x10 -> x0, blocking collectives: 145 us -> none  [apply_op(): x_col = lax.all_gather(x_moved, 'row', axis=0, tiled=True)]
    dot_general x44 -> x6, matrix products: 89.2 us -> 3.85 us  [local_program(): lax.dot_general(x, z[:, t * LN:(t + 1) * LN], ROW_CONTRACT, precision=HI,...]
    ppermute x10 -> x3, waiting for transfers between devices: 61.2 us -> 0.01 us  [the longest x1 0.01 us: local_program(): lh = lax.ppermute(left_start.astype(jnp.bfloat16), grid_axes, to_cols)]
    ppermute x10 -> x3, starting transfers between devices: 41.8 us -> 10.7 us  [the longest x1 5.1 us: local_program(): lh = lax.ppermute(left_start.astype(jnp.bfloat16), grid_axes, to_cols)]
  transfers between devices with their start and end apart: 29 -> 3, of which waited for: 24 -> 0; matrix products, arithmetic and copies ran while one was open for 2% -> 1% of each run, Pallas kernels for 0% -> 8%
where the time goes in v2:
time: 616 us; the launch traced here: 613 us
  Pallas kernels  562 us (91%)
  local copies, waits for them, and re-layouts  27.1 us (4%)
  starting transfers between devices  10.7 us (2%)
  loops' own time  7.98 us (1%)
    pallas_call x9, Pallas kernels, grid_total(): pl.pallas_call(total_kernel, out_shape=jax.ShapeDtypeStruct(g.shape, f32)...  215 us
    pallas_call x5, Pallas kernels, apply_pair(): pl.pallas_call(functools.partial(apply_kernel, left_across), out_shape=(j...  177 us
    pallas_call x8, Pallas kernels, orth(): pl.pallas_call(functools.partial(orth_second if last else orth_first, sca...  171 us
    while x32, local copies, waits for them, and re-layouts  12.9 us
    unnamed x15, local copies, waits for them, and re-layouts  12.6 us
  transfers between devices with their start and end apart: 3, of which 0 were waited for; matrix products, arithmetic and copies ran while one was open for 1% of the time, Pallas kernels for 8%

profile of v2, /device:TPU:97, one launch (start us, length us, event | category | flops | bytes accessed | tf_op | source)
XLA Modules:
  0.0 612.9 jit_solution(5893666174607617740)
XLA Ops:
  0.6 1.0 copy.42
  1.6 1.1 copy.43
  2.7 5.1 collective-permute-start
  7.8 0.3 copy.13
  8.1 0.0 copy-done.11
  8.1 6.5 %copy.12 = bf16[2048,1024]{0,1:T(8,128)(2,1)} copy(bf16[2048,1024]{1,0:T(8,128)(2,1)} %param.8) | data formatting | bytes 8388608 | tf_op args[2]
  14.6 0.0 collective-permute-done
  14.6 508.0 %while.16 = (s32[]{:T(128)}, f32[96,384]{1,0:T(8,128)}, f32[256,384]{1,0:T(8,128)}, bf16[96,384]{1,0:T(8,128)(2,1)S(1)}, bf16[256,384]{1,0:T(8,128)(2,1)S(1)}, /...) while((s32[]{:T(128)}, f32[96,384]{1,0:T(8,128)}, ...), condition=%wide.region_1.0_spmd, body=%wide.region_0.0_spmd.sunk | while | flops 2 | bytes 11698501 | solution.py:421
  14.7 34.9 %apply_n.3 = (f32[96,384]{1,0:T(8,128)S(1)}, f32[256,384]{1,0:T(8,128)S(1)}, f32[1536,128]{1,0:T(8,128)S(1)}) custom-call(bf16[768,384]{1,0:T(8,128)(2,1)S(1)} %get-tuple-element.214.lop, bf16[96,384]{1,0:T(8,128)(2,1)S(1)} %get-tuple-element.202.lx, bf16[1024,2048]{1,0:T(8,128)(2,1)} %get-tuple-element.215.rop, bf16[256,384]{1,0:T(8,128)(2,1)S(1)} %get-tuple-element.203.rx), custom_call_target="tpu_custom_call" | custom-call | tf_op jit(solution)/shard_map/while/body/eval_jaxpr/apply_n/pallas_call | solution.py:337
  49.7 0.9 copy-done
  50.6 0.7 copy-done.2
  51.3 0.7 copy-done.5
  52.0 24.2 %grid_total.6.g_ref = f32[1536,128]{1,0:T(8,128)} custom-call(f32[1536,128]{1,0:T(8,128)} %copy-done), custom_call_target="tpu_custom_call" | custom-call | tf_op jit(solution)/shard_map/while/body/eval_jaxpr/grid_total/pallas_call | solution.py:188
  76.2 22.1 %orth_first.2 = (f32[96,384]{1,0:T(8,128)}, f32[256,384]{1,0:T(8,128)}, f32[1536,128]{1,0:T(8,128)}) custom-call(f32[1536,128]{1,0:T(8,128)} %grid_total.6.g_ref, f32[96,384]{1,0:T(8,128)} %copy-done.5, f32[256,384]{1,0:T(8,128)} %copy-done.2), custom_call_target="tpu_custom_call" | custom-call | tf_op jit(solution)/shard_map/while/body/eval_jaxpr/orth_first/pallas_call | solution.py:390
  98.2 23.0 %grid_total.7.g_ref = f32[1536,128]{1,0:T(8,128)} custom-call(f32[1536,128]{1,0:T(8,128)} %get-tuple-element.174.g_ref), custom_call_target="tpu_custom_call" | custom-call | tf_op jit(solution)/shard_map/while/body/eval_jaxpr/grid_total/pallas_call | solution.py:188
  121.2 20.8 %orth_second.2 = (f32[96,384]{1,0:T(8,128)}, f32[256,384]{1,0:T(8,128)}, bf16[96,384]{1,0:T(8,128)(2,1)}, bf16[256,384]{1,0:T(8,128)(2,1)}) custom-call(f32[1536,128]{1,0:T(8,128)} %grid_total.7.g_ref, f32[96,384]{1,0:T(8,128)} %get-tuple-element.175.ly, f32[256,384]{1,0:T(8,128)} %get-tuple-element.176.ry), custom_call_target="tpu_custom_call" | custom-call | tf_op jit(solution)/shard_map/while/body/eval_jaxpr/orth_second/pallas_call | solution.py:390
  142.1 0.9 copy-done.4
  143.0 0.9 copy-done.7
  143.9 32.1 %apply_t.1 = (f32[96,384]{1,0:T(8,128)S(1)}, f32[256,384]{1,0:T(8,128)S(1)}, f32[1536,128]{1,0:T(8,128)S(1)}) custom-call(bf16[384,768]{1,0:T(8,128)(2,1)S(1)} %get-tuple-element.216.lop, bf16[96,384]{1,0:T(8,128)(2,1)S(1)} %copy-done.7, bf16[2048,1024]{1,0:T(8,128)(2,1)} %get-tuple-element.217.rop, bf16[256,384]{1,0:T(8,128)(2,1)S(1)} %copy-done.4), custom_call_target="tpu_custom_call" | custom-call | tf_op jit(solution)/shard_map/while/body/eval_jaxpr/apply_t/pallas_call | solution.py:337
  176.0 0.9 copy-done.1
  176.9 0.7 copy-done.3
  177.7 0.7 copy-done.6
  178.3 23.5 %grid_total.8.g_ref = f32[1536,128]{1,0:T(8,128)} custom-call(f32[1536,128]{1,0:T(8,128)} %copy-done.1), custom_call_target="tpu_custom_call" | custom-call | tf_op jit(solution)/shard_map/while/body/eval_jaxpr/grid_total/pallas_call | solution.py:188
  201.9 22.0 %orth_first.3 = (f32[96,384]{1,0:T(8,128)}, f32[256,384]{1,0:T(8,128)}, f32[1536,128]{1,0:T(8,128)}) custom-call(f32[1536,128]{1,0:T(8,128)} %grid_total.8.g_ref, f32[96,384]{1,0:T(8,128)} %copy-done.6, f32[256,384]{1,0:T(8,128)} %copy-done.3), custom_call_target="tpu_custom_call" | custom-call | tf_op jit(solution)/shard_map/while/body/eval_jaxpr/orth_first/pallas_call | solution.py:390
  223.9 22.8 %grid_total.9.g_ref = f32[1536,128]{1,0:T(8,128)} custom-call(f32[1536,128]{1,0:T(8,128)} %get-tuple-element.182.g_ref), custom_call_target="tpu_custom_call" | custom-call | tf_op jit(solution)/shard_map/while/body/eval_jaxpr/grid_total/pallas_call | solution.py:188
  246.7 20.5 %orth_second.3 = (f32[96,384]{1,0:T(8,128)}, f32[256,384]{1,0:T(8,128)}, bf16[96,384]{1,0:T(8,128)(2,1)S(1)}, bf16[256,384]{1,0:T(8,128)(2,1)S(1)}) custom-call(f32[1536,128]{1,0:T(8,128)} %grid_total.9.g_ref, f32[96,384]{1,0:T(8,128)} %get-tuple-element.183.ly, f32[256,384]{1,0:T(8,128)} %get-tuple-element.184.ry), custom_call_target="tpu_custom_call" | custom-call | tf_op jit(solution)/shard_map/while/body/eval_jaxpr/orth_second/pallas_call | solution.py:390
  267.6 31.1 %apply_n.3 = (f32[96,384]{1,0:T(8,128)S(1)}, f32[256,384]{1,0:T(8,128)S(1)}, f32[1536,128]{1,0:T(8,128)S(1)}) custom-call(bf16[768,384]{1,0:T(8,128)(2,1)S(1)} %get-tuple-element.214.lop, bf16[96,384]{1,0:T(8,128)(2,1)S(1)} %get-tuple-element.202.lx, bf16[1024,2048]{1,0:T(8,128)(2,1)} %get-tuple-element.215.rop, bf16[256,384]{1,0:T(8,128)(2,1)S(1)} %get-tuple-element.203.rx), custom_call_target="tpu_custom_call" | custom-call | tf_op jit(solution)/shard_map/while/body/eval_jaxpr/apply_n/pallas_call | solution.py:337
  298.7 0.9 copy-done
  299.6 0.7 copy-done.2
  300.3 0.7 copy-done.5
  301.0 23.5 %grid_total.6.g_ref = f32[1536,128]{1,0:T(8,128)} custom-call(f32[1536,128]{1,0:T(8,128)} %copy-done), custom_call_target="tpu_custom_call" | custom-call | tf_op jit(solution)/shard_map/while/body/eval_jaxpr/grid_total/pallas_call | solution.py:188
  324.5 21.7 %orth_first.2 = (f32[96,384]{1,0:T(8,128)}, f32[256,384]{1,0:T(8,128)}, f32[1536,128]{1,0:T(8,128)}) custom-call(f32[1536,128]{1,0:T(8,128)} %grid_total.6.g_ref, f32[96,384]{1,0:T(8,128)} %copy-done.5, f32[256,384]{1,0:T(8,128)} %copy-done.2), custom_call_target="tpu_custom_call" | custom-call | tf_op jit(solution)/shard_map/while/body/eval_jaxpr/orth_first/pallas_call | solution.py:390
  346.2 22.9 %grid_total.7.g_ref = f32[1536,128]{1,0:T(8,128)} custom-call(f32[1536,128]{1,0:T(8,128)} %get-tuple-element.174.g_ref), custom_call_target="tpu_custom_call" | custom-call | tf_op jit(solution)/shard_map/while/body/eval_jaxpr/grid_total/pallas_call | solution.py:188
  369.1 21.0 %orth_second.2 = (f32[96,384]{1,0:T(8,128)}, f32[256,384]{1,0:T(8,128)}, bf16[96,384]{1,0:T(8,128)(2,1)}, bf16[256,384]{1,0:T(8,128)(2,1)}) custom-call(f32[1536,128]{1,0:T(8,128)} %grid_total.7.g_ref, f32[96,384]{1,0:T(8,128)} %get-tuple-element.175.ly, f32[256,384]{1,0:T(8,128)} %get-tuple-element.176.ry), custom_call_target="tpu_custom_call" | custom-call | tf_op jit(solution)/shard_map/while/body/eval_jaxpr/orth_second/pallas_call | solution.py:390
  390.1 0.9 copy-done.4
  391.1 0.9 copy-done.7
  391.9 32.1 %apply_t.1 = (f32[96,384]{1,0:T(8,128)S(1)}, f32[256,384]{1,0:T(8,128)S(1)}, f32[1536,128]{1,0:T(8,128)S(1)}) custom-call(bf16[384,768]{1,0:T(8,128)(2,1)S(1)} %get-tuple-element.216.lop, bf16[96,384]{1,0:T(8,128)(2,1)S(1)} %copy-done.7, bf16[2048,1024]{1,0:T(8,128)(2,1)} %get-tuple-element.217.rop, bf16[256,384]{1,0:T(8,128)(2,1)S(1)} %copy-done.4), custom_call_target="tpu_custom_call" | custom-call | tf_op jit(solution)/shard_map/while/body/eval_jaxpr/apply_t/pallas_call | solution.py:337
  424.1 0.9 copy-done.1
  425.0 0.7 copy-done.3
  425.7 0.7 copy-done.6
  426.4 23.6 %grid_total.8.g_ref = f32[1536,128]{1,0:T(8,128)} custom-call(f32[1536,128]{1,0:T(8,128)} %copy-done.1), custom_call_target="tpu_custom_call" | custom-call | tf_op jit(solution)/shard_map/while/body/eval_jaxpr/grid_total/pallas_call | solution.py:188
  450.0 21.7 %orth_first.3 = (f32[96,384]{1,0:T(8,128)}, f32[256,384]{1,0:T(8,128)}, f32[1536,128]{1,0:T(8,128)}) custom-call(f32[1536,128]{1,0:T(8,128)} %grid_total.8.g_ref, f32[96,384]{1,0:T(8,128)} %copy-done.6, f32[256,384]{1,0:T(8,128)} %copy-done.3), custom_call_target="tpu_custom_call" | custom-call | tf_op jit(solution)/shard_map/while/body/eval_jaxpr/orth_first/pallas_call | solution.py:390
  471.7 22.8 %grid_total.9.g_ref = f32[1536,128]{1,0:T(8,128)} custom-call(f32[1536,128]{1,0:T(8,128)} %get-tuple-element.182.g_ref), custom_call_target="tpu_custom_call" | custom-call | tf_op jit(solution)/shard_map/while/body/eval_jaxpr/grid_total/pallas_call | solution.py:188
  494.5 20.7 %orth_second.3 = (f32[96,384]{1,0:T(8,128)}, f32[256,384]{1,0:T(8,128)}, bf16[96,384]{1,0:T(8,128)(2,1)S(1)}, bf16[256,384]{1,0:T(8,128)(2,1)S(1)}) custom-call(f32[1536,128]{1,0:T(8,128)} %grid_total.9.g_ref, f32[96,384]{1,0:T(8,128)} %get-tuple-element.183.ly, f32[256,384]{1,0:T(8,128)} %get-tuple-element.184.ry), custom_call_target="tpu_custom_call" | custom-call | tf_op jit(solution)/shard_map/while/body/eval_jaxpr/orth_second/pallas_call | solution.py:390
  522.6 3.3 collective-permute-start.1
  526.0 2.3 collective-permute-start.2
  528.3 46.4 %apply_n.2 = (f32[96,384]{1,0:T(8,128)S(1)}, f32[256,384]{1,0:T(8,128)S(1)}, f32[1536,128]{1,0:T(8,128)}) custom-call(bf16[768,384]{1,0:T(8,128)(2,1)S(1)} %get-tuple-element.228, bf16[96,384]{1,0:T(8,128)(2,1)S(1)} %get-tuple-element.73.lx, bf16[1024,2048]{1,0:T(8,128)(2,1)} %get-tuple-element.227, bf16[256,384]{1,0:T(8,128)(2,1)S(1)} %get-tuple-element.74.rx), custom_call_target="tpu_custom_call" | custom-call | tf_op jit(solution)/shard_map/apply_n/pallas_call | solution.py:337
  574.7 0.0 collective-permute-done.1
  574.7 0.5 convolution_dynamic-update-slice_fusion.2
  575.2 0.5 convolution_dynamic-update-slice_fusion.1
  575.7 0.5 convolution_dynamic-update-slice_fusion
  576.2 0.0 collective-permute-done.2
  576.2 0.8 convolution_dynamic-update-slice_fusion.5
  577.0 0.8 convolution_dynamic-update-slice_fusion.4
  577.8 0.8 convolution_dynamic-update-slice_fusion.3
  578.6 1.1 copy-done.9
  579.7 28.5 %grid_total.5 = f32[2560,128]{1,0:T(8,128)} custom-call(f32[2560,128]{1,0:T(8,128)} %copy-done.9), custom_call_target="tpu_custom_call" | custom-call | tf_op jit(solution)/shard_map/grid_total/pallas_call | solution.py:188
  608.1 0.0 slice-start
  608.1 1.3 slice-done
  609.4 0.4 copy.14
  609.8 0.1 slice_multiply_fusion
  609.9 1.1 copy.16
  610.9 1.0 copy.15
  612.0 0.7 copy.45
  (25 shorter events, 0.1 us)
Async XLA Ops:
  0.6 7.2 %copy-start.8 = (bf16[768,384]{1,0:T(8,128)(2,1)S(1)}, bf16[768,384]{1,0:T(8,128)(2,1)}, u32[]{:S(2)}) copy-start(bf16[768,384]{1,0:T(8,128)(2,1)} %lop.1) | copy-start | bytes 1769476
  1.6 6.5 %copy-start.11 = (f32[96,384]{1,0:T(8,128)}, f32[96,384]{1,0:T(8,128)S(1)}, u32[]{:S(2)}) copy-start(f32[96,384]{1,0:T(8,128)S(1)} %copy.42) | copy-start | bytes 442372
  2.7 12.0 %copy-start.10 = (f32[256,384]{1,0:T(8,128)}, f32[256,384]{1,0:T(8,128)S(1)}, u32[]{:S(2)}) copy-start(f32[256,384]{1,0:T(8,128)S(1)} %copy.43) | copy-start | bytes 1179652
  2.7 11.9 %collective-permute-start = (bf16[96,384]{1,0:T(8,128)(2,1)S(1)}, bf16[96,384]{1,0:T(8,128)(2,1)S(1)}, u32[]{:S(2)}, u32[]{:S(2)}) collective-permute-start(bf16[96,384]{1,0:T(8,128)(2,1)S(1)} %convert_element_type.6), channel_id=1, source_target_pairs={{0,0},{1,8},{2,16},{3,24},{4,1},{5,9},{6,17},{7,25},{8,2},{9,10},{... | collective-permute-start | bytes 221192 | tf_op jit(solution)/shard_map/ppermute | solution.py:419
  49.7 0.9 copy-start
  50.6 0.7 copy-start.2
  51.3 0.7 copy-start.5
  142.1 0.9 copy-start.4
  143.0 0.9 copy-start.7
  176.0 0.9 copy-start.1
  176.9 0.7 copy-start.3
  177.7 0.7 copy-start.6
  298.7 0.9 copy-start
  299.6 0.7 copy-start.2
  300.3 0.7 copy-start.5
  390.1 0.9 copy-start.4
  391.1 0.9 copy-start.7
  424.1 0.9 copy-start.1
  425.0 0.7 copy-start.3
  425.7 0.7 copy-start.6
  522.6 52.1 %collective-permute-start.1 = (f32[96,384]{1,0:T(8,128)}, f32[96,384]{1,0:T(8,128)S(1)}, u32[]{:S(2)}, u32[]{:S(2)}) collective-permute-start(f32[96,384]{1,0:T(8,128)} %get-tuple-element.72), channel_id=1, source_target_pairs={{0,0},{8,1},{16,2},{24,3},{1,4},{9,5},{17,6},{25,7},{2,8},{10,9},{... | collective-permute-start | bytes 442376 | tf_op jit(solution)/shard_map/ppermute | solution.py:422
  526.0 50.2 %collective-permute-start.2 = (f32[256,384]{1,0:T(8,128)}, f32[256,384]{1,0:T(8,128)S(1)}, u32[]{:S(2)}, u32[]{:S(2)}) collective-permute-start(f32[256,384]{1,0:T(8,128)} %get-tuple-element.225), channel_id=1, source_target_pairs={{0,0},{1,8},{2,16},{3,24},{4,1},{5,9},{6,17},{7,25},{8,2},{9,10},{... | collective-permute-start | bytes 1179656 | tf_op jit(solution)/shard_map/ppermute | solution.py:423
  578.6 1.1 copy-start.9
  608.1 1.3 slice-start
